TPU v7x, 8 devices: a whole 2x2x1 slice. The times are simulated.
8 devices in a mesh: dp: 1 (over z), tp: 8 (over y, x, core).
Axes of the slice: x: 2, y: 2, z: 1, core: 2. Of those that a mesh axis runs over, the one named last changes fastest.
Arguments:
- x: bfloat16 [24, 384, 5120], P('dp')
- seq_lens: int32 [24], P('dp')
- w_query: bfloat16 [5120, 5120], P(None, 'tp')
- w_key: bfloat16 [5120, 1024], P(None, 'tp')
- w_value: bfloat16 [5120, 1024], P(None, 'tp')
- w_out: bfloat16 [5120, 5120], P('tp')
- w_gate: bfloat16 [5120, 27648], P(None, 'tp')
- w_up: bfloat16 [5120, 27648], P(None, 'tp')
- w_down: bfloat16 [27648, 5120], P('tp')
- attn_gain: bfloat16 [5120], replicated
- mlp_gain: bfloat16 [5120], replicated
- k_cache: bfloat16 [24, 768, 8, 128], P('dp', None, 'tp')
- v_cache: bfloat16 [24, 768, 8, 128], P('dp', None, 'tp')
Outputs:
- output 1: bfloat16 [24, 384, 5120], P('dp')
- output 2: bfloat16 [24, 768, 8, 128], P('dp', None, 'tp')
- output 3: bfloat16 [24, 768, 8, 128], P('dp', None, 'tp')
All inputs are finite; a program needn't handle non-finite values.
Results may differ from a plain program's by a relative error of at most 0.0114497.
Values are sent between devices in bfloat16 or wider.
A program may use at most 1.25 GiB of HBM per device.

v0:
```python
import jax
import jax.numpy as jnp
from jax import lax
from jax.sharding import PartitionSpec as P

EPS = 1e-5
ROPE_BASE = 10000.0


def rms_norm(rows, gain):
    rows32 = rows.astype(jnp.float32)
    inv_rms = lax.rsqrt(jnp.mean(rows32 * rows32, axis=-1, keepdims=True) + EPS)
    return (rows32 * inv_rms * gain.astype(jnp.float32)).astype(jnp.bfloat16)


def rotary(vecs):
    seq_len = vecs.shape[1]
    head_dim = vecs.shape[-1]
    half_dim = head_dim // 2
    inv_freq = ROPE_BASE ** (-jnp.arange(0, head_dim, 2).astype(jnp.float32) / head_dim)
    angles = jnp.arange(seq_len).astype(jnp.float32)[:, None] * inv_freq[None, :]
    table_shape = (1, seq_len) + (1,) * (vecs.ndim - 3) + (half_dim,)
    cos_tab = jnp.cos(angles).reshape(table_shape)
    sin_tab = jnp.sin(angles).reshape(table_shape)
    pairs = vecs.reshape(vecs.shape[:-1] + (half_dim, 2))
    even_part = pairs[..., 0]
    odd_part = pairs[..., 1]
    turned = jnp.stack([even_part * cos_tab - odd_part * sin_tab, even_part * sin_tab + odd_part * cos_tab], axis=-1)
    return turned.reshape(vecs.shape).astype(jnp.bfloat16)


def causal_attention(queries, keys, values, seq_lens):
    seq_len = queries.shape[1]
    head_dim = queries.shape[-1]
    scores = jnp.einsum("bqkgh,bskh->bkgqs", queries, keys, preferred_element_type=jnp.float32) * head_dim ** -0.5
    positions = jnp.arange(seq_len)
    allowed = (positions[None, None, :] <= positions[None, :, None]) & (positions[None, None, :] < seq_lens[:, None, None])
    scores = jnp.where(allowed[:, None, None], scores, -jnp.inf)
    probs = jax.nn.softmax(scores, axis=-1).astype(jnp.bfloat16)
    return jnp.einsum("bkgqs,bskh->bqkgh", probs, values, preferred_element_type=jnp.float32).astype(jnp.bfloat16)


def sum_partials(partial, resid_rows, tp_size):
    batch_size, seq_len, model_width = partial.shape
    stacked = partial.reshape(batch_size, tp_size, seq_len // tp_size, model_width)
    received = lax.all_to_all(stacked, "tp", 1, 1, tiled=True)
    summed = jnp.sum(received.astype(jnp.float32), axis=1)
    return (resid_rows.astype(jnp.float32) + summed).astype(jnp.bfloat16)


def solution(mesh):
    tp_size = mesh.shape["tp"]

    def layer_shard(x, seq_lens, w_query, w_key, w_value, w_out, w_gate, w_up, w_down, attn_gain, mlp_gain, k_cache, v_cache):
        batch_size, seq_len, model_width = x.shape
        head_dim = k_cache.shape[3]
        kv_local = k_cache.shape[2]
        group_size = w_query.shape[1] // (head_dim * kv_local)
        rows_each = seq_len // tp_size
        tp_index = lax.axis_index("tp")
        normed = rms_norm(x, attn_gain)
        queries = rotary(jnp.einsum("bsd,dk->bsk", normed, w_query, preferred_element_type=jnp.float32).reshape(batch_size, seq_len, kv_local, group_size, head_dim))
        keys = rotary(jnp.einsum("bsd,dk->bsk", normed, w_key, preferred_element_type=jnp.float32).reshape(batch_size, seq_len, kv_local, head_dim))
        values = jnp.einsum("bsd,dk->bsk", normed, w_value, preferred_element_type=jnp.float32).astype(jnp.bfloat16).reshape(batch_size, seq_len, kv_local, head_dim)
        valid = (jnp.arange(seq_len)[None, :] < seq_lens[:, None])[:, :, None, None]
        keys = jnp.where(valid, keys, jnp.zeros_like(keys))
        values = jnp.where(valid, values, jnp.zeros_like(values))
        k_cache_out = lax.dynamic_update_slice(k_cache, keys, (0, 0, 0, 0))
        v_cache_out = lax.dynamic_update_slice(v_cache, values, (0, 0, 0, 0))
        attn_rows = causal_attention(queries, keys, values, seq_lens).reshape(batch_size, seq_len, -1)
        attn_part = jnp.einsum("bsk,kd->bsd", attn_rows, w_out, preferred_element_type=jnp.float32).astype(jnp.bfloat16)
        x_rows = lax.dynamic_slice_in_dim(x, tp_index * rows_each, rows_each, axis=1)
        hidden_rows = sum_partials(attn_part, x_rows, tp_size)
        normed_mlp = lax.all_gather(rms_norm(hidden_rows, mlp_gain), "tp", axis=1, tiled=True)
        gate_pre = jnp.einsum("bsd,df->bsf", normed_mlp, w_gate, preferred_element_type=jnp.float32)
        up_pre = jnp.einsum("bsd,df->bsf", normed_mlp, w_up, preferred_element_type=jnp.float32)
        gated = (jax.nn.silu(gate_pre) * up_pre).astype(jnp.bfloat16)
        mlp_part = jnp.einsum("bsf,fd->bsd", gated, w_down, preferred_element_type=jnp.float32).astype(jnp.bfloat16)
        out_rows = sum_partials(mlp_part, hidden_rows, tp_size)
        y = lax.all_gather(out_rows, "tp", axis=1, tiled=True)
        return y, k_cache_out, v_cache_out

    cache_spec = P("dp", None, "tp", None)
    return jax.shard_map(layer_shard, mesh=mesh, in_specs=(P("dp", None, None), P("dp"), P(None, "tp"), P(None, "tp"), P(None, "tp"), P("tp", None), P(None, "tp"), P(None, "tp"), P("tp", None), P(), P(), cache_spec, cache_spec), out_specs=(P("dp", None, None), cache_spec, cache_spec), check_vma=False)
```

profile of v0, /device:TPU:0, one launch (start us, length us, event | category | flops | bytes accessed | tf_op | source)
XLA Modules:
  0.0 4742.0 jit_solution(15524830903913959384)
XLA Ops:
  7.2 0.0 copy-start
  7.2 5.1 copy.67
  12.3 5.0 copy.66
  17.3 0.7 iota_compare_fusion
  18.0 29.1 fusion
  47.2 0.0 copy-done.12
  47.2 37.9 fusion.9
  85.1 5.1 copy.56
  90.1 0.4 multiply_cosine_fusion
  90.6 0.7 multiply_subtract_fusion
  91.2 1.6 maximum_convert_fusion
  92.9 4.6 copy.38
  97.4 83.4 %fusion.7 = f32[24,384,640]{2,1,0:T(8,128)} fusion(bf16[24,384,5120]{2,1,0:T(8,128)(2,1)} %param.13, f32[5120]{0:T(1024)S(1)} %convert_element_type.129, f32[24,384]{1,0:T(8,128)S(1)} %add_rsqrt_fusion, bf16[5120,640]{1,0:T(8,128)(2,1)} %param.15), kind=kOutput, calls=%fused_computation.16 | convolution fusion | flops 60586721280 | bytes 124575744 | tf_op jit(solution)/shard_map/bsd,dk->bsk/dot_general | solution.py:62
  180.9 24.5 copy.39
  205.4 9.8 subtract_convert_fusion
  215.3 0.1 iota_compare_fusion.1
  215.4 5.6 pad_maximum_fusion
  221.0 2.1 broadcast_and_fusion
  223.1 31.7 fusion.5
  254.8 23.6 fusion.4
  278.4 36.6 bitcast_dynamic-update-slice_fusion
  315.0 32.5 fusion.27
  347.5 83.6 %convolution_convert_fusion = bf16[24,384,5120]{2,1,0:T(8,128)(2,1)} fusion(bf16[24,384,640]{1,2,0:T(8,128)(2,1)} %bitcast.83, bf16[640,5120]{1,0:T(8,128)(2,1)} %param.18), kind=kOutput, calls=%fused_computation.15 | convolution fusion | flops 60445163520 | bytes 112721920 | tf_op jit(solution)/shard_map/bsk,kd->bsd/dot_general | solution.py:71
  431.1 61.1 %copy.44 = bf16[24,8,48,5120]{3,2,0,1:T(8,128)(2,1)} copy(bf16[24,8,48,5120]{3,2,1,0:T(8,128)(2,1)} %bitcast.16) | data formatting | bytes 188743680 | tf_op jit(solution)/shard_map/reshape | solution.py:45
  492.2 10.6 all-to-all-start
  502.8 0.0 all-gather.3.cloned.1.call-start
  502.9 1017.1 %all-to-all-done = bf16[24,8,48,5120]{3,2,0,1:T(8,128)(2,1)} async-done(((bf16[24,8,48,5120]{3,2,0,1:T(8,128)(2,1)}), bf16[24,8,48,5120]{3,2,0,1:T(8,128)(2,1)}, u32[]{:S(2)}, u32[]{:S(2)}) %all-to-all-start) | async-done | bytes 94371872 | tf_op jit(solution)/shard_map/all_to_all | solution.py:46
  1520.1 51.5 %convert_reduce_fusion.1 = f32[24,48,5120]{2,1,0:T(8,128)S(1)} fusion(bf16[24,8,48,5120]{3,2,0,1:T(8,128)(2,1)} %all-to-all-done), kind=kLoop, calls=%fused_computation.6 | loop fusion | flops 88473600 | bytes 117964800 | tf_op jit(solution)/shard_map/reduce_sum | solution.py:47
  1571.5 8.3 fusion.21
  1579.9 4.2 copy-done.2
  1584.1 6.2 fusion.23
  1590.3 0.0 all-gather.3.cloned.1.call-update
  1590.3 0.0 all-gather.5.cloned.1.call-start
  1590.4 412.5 %all-gather.3.cloned.1.call-done = bf16[24,384,5120]{2,1,0:T(8,128)(2,1)} async-done(((bf16[24,48,5120]{2,1,0:T(8,128)(2,1)}), bf16[24,384,5120]{2,1,0:T(8,128)(2,1)}) %all-gather.3.cloned.1.call-update) | async-done | bytes 94371856 | tf_op jit(solution)/shard_map/all_gather | solution.py:74
  2002.9 356.9 %fusion.14 = f32[24,384,3456]{2,1,0:T(8,128)} fusion(bf16[24,384,5120]{2,1,0:T(8,128)(2,1)} %all-gather.3.cloned.1.call-done, bf16[5120,3456]{1,0:T(8,128)(2,1)} %param.20), kind=kOutput, calls=%fused_computation.20 | convolution fusion | flops 326149079040 | bytes 257163264 | tf_op jit(solution)/shard_map/bsd,df->bsf/dot_general | solution.py:76
  2359.8 356.5 %fusion.16 = f32[24,384,3456]{2,1,0:T(8,128)} fusion(bf16[24,384,5120]{2,1,0:T(8,128)(2,1)} %all-gather.3.cloned.1.call-done, bf16[5120,3456]{1,0:T(8,128)(2,1)} %param.19), kind=kOutput, calls=%fused_computation.22 | convolution fusion | flops 326149079040 | bytes 257163264 | tf_op jit(solution)/shard_map/bsd,df->bsf/dot_general | solution.py:75
  2716.3 371.5 %fusion.6 = bf16[24,384,5120]{2,1,0:T(8,128)(2,1)} fusion(f32[24,384,3456]{2,1,0:T(8,128)} %fusion.14, f32[24,384,3456]{2,1,0:T(8,128)} %fusion.16, bf16[3456,5120]{1,0:T(8,128)(2,1)} %param.21), kind=kOutput, calls=%fused_computation.14 | convolution fusion | flops 326387367936 | bytes 384565248 | tf_op jit(solution)/shard_map/bsf,fd->bsd/dot_general | solution.py:78
  3087.8 61.0 %copy.45 = bf16[24,8,48,5120]{3,2,0,1:T(8,128)(2,1)} copy(bf16[24,8,48,5120]{3,2,1,0:T(8,128)(2,1)} %bitcast.20) | data formatting | bytes 188743680 | tf_op jit(solution)/shard_map/reshape | solution.py:45
  3148.8 1039.0 %all_to_all.10 = bf16[24,8,48,5120]{3,2,0,1:T(8,128)(2,1)} all-to-all(bf16[24,8,48,5120]{3,2,0,1:T(8,128)(2,1)} %copy.45), channel_id=1, replica_groups=mesh['dp'=1,'tp'=8] {'tp'}, dimensions={1} | all-to-all | bytes 188743680 | tf_op jit(solution)/shard_map/all_to_all | solution.py:46
  4187.8 59.2 %convert_reduce_fusion = f32[24,48,5120]{2,1,0:T(8,128)} fusion(bf16[24,8,48,5120]{3,2,0,1:T(8,128)(2,1)} %all_to_all.10), kind=kLoop, calls=%fused_computation.5 | loop fusion | flops 88473600 | bytes 117964800 | tf_op jit(solution)/shard_map/reduce_sum | solution.py:47
  4247.1 0.0 slice-done.2
  4247.1 13.7 fusion.24
  4260.8 0.0 all-gather.5.cloned.1.call-update
  4260.8 1.6 broadcast_select_fusion
  4262.5 3.2 copy.46
  4265.7 1.8 constant_dynamic-update-slice_fusion
  4267.5 405.2 %all-gather.5.cloned.1.call-done = bf16[24,384,5120]{2,1,0:T(8,128)(2,1)} async-done(((bf16[24,48,5120]{2,1,0:T(8,128)(2,1)}), bf16[24,384,5120]{2,1,0:T(8,128)(2,1)}) %all-gather.5.cloned.1.call-update) | async-done | bytes 94371856 | tf_op jit(solution)/shard_map/all_gather | solution.py:80
  4672.7 61.9 %copy.68 = bf16[24,384,5120]{2,1,0:T(8,128)(2,1)} copy(bf16[24,384,5120]{2,1,0:T(8,128)(2,1)} %all-gather.5.cloned.1.call-done) | data formatting | bytes 188743680
  (35 shorter events, 0.1 us)
Async XLA Ops:
  7.2 271.3 %copy-start = (bf16[5120,128]{1,0:T(8,128)(2,1)S(1)}, bf16[5120,128]{1,0:T(8,128)(2,1)}, u32[]{:S(2)}) copy-start(bf16[5120,128]{1,0:T(8,128)(2,1)} %param.17) | copy-start | bytes 3932164
  18.0 29.2 copy-start.9
  18.0 29.2 copy-start.12
  205.4 9.9 copy-start.11
  205.4 15.6 copy-start.6
  205.4 17.7 copy-start.5
  215.4 63.1 %copy-start.7 = (pred[24,384]{1,0:T(8,128)(4,1)}, pred[24,384]{1,0:T(8,128)(4,1)S(1)}, u32[]{:S(2)}) copy-start(pred[24,384]{1,0:T(8,128)(4,1)S(1)} %iota_compare_fusion.1) | copy-start | bytes 27652
  223.1 31.8 copy-start.4
  492.2 10.7 copy-start.10
  492.2 1027.9 %all-to-all-start = ((bf16[24,8,48,5120]{3,2,0,1:T(8,128)(2,1)}), bf16[24,8,48,5120]{3,2,0,1:T(8,128)(2,1)}, u32[]{:S(2)}, u32[]{:S(2)}) async-start(bf16[24,8,48,5120]{3,2,0,1:T(8,128)(2,1)} %copy.44), calls=%async_computation | async-start | bytes 188743680 | tf_op jit(solution)/shard_map/all_to_all | solution.py:46
  502.8 1500.0 %all-gather.3.cloned.1.call-start = ((), (), s32[]{:S(2)}) async-start(), calls=%async_computation.2 | async-start | bytes 106168320 | tf_op jit(solution)/shard_map/all_gather | solution.py:74
  1579.9 4.3 copy-start.2
  1590.3 3082.4 %all-gather.5.cloned.1.call-start = ((), (), s32[]{:S(2)}) async-start(), calls=%async_computation.3 | async-start | bytes 106168320 | tf_op jit(solution)/shard_map/all_gather | solution.py:80
  3148.8 1098.2 %slice-start = ((s8[11796480]{0:T(1024)(128)(4,1)}), s8[4194304]{0:T(1024)(128)(4,1)S(1)}, s32[]{:S(2)}) async-start(s8[11796480]{0:T(1024)(128)(4,1)} %bitcast.76), calls=%async_computation.4 | async-start | bytes 8388608
  3148.8 1098.2 %slice-start.1 = ((s8[11796480]{0:T(1024)(128)(4,1)}), s8[4194304]{0:T(1024)(128)(4,1)S(1)}, s32[]{:S(2)}) async-start(s8[11796480]{0:T(1024)(128)(4,1)} %bitcast.76), calls=%async_computation.5 | async-start | bytes 8388608
  4187.8 59.2 %slice-start.2 = ((s8[11796480]{0:T(1024)(128)(4,1)}), s8[3407872]{0:T(1024)(128)(4,1)S(1)}, s32[]{:S(2)}) async-start(s8[11796480]{0:T(1024)(128)(4,1)} %bitcast.76), calls=%async_computation.6 | async-start | bytes 6815744
  4247.1 13.7 copy-start.3
  4247.1 13.7 copy-start.8
  4672.7 61.9 %copy-start.1 = (bf16[5120,128]{1,0:T(8,128)(2,1)S(1)}, bf16[5120,128]{1,0:T(8,128)(2,1)}, u32[]{:S(2)}) copy-start(bf16[5120,128]{1,0:T(8,128)(2,1)} %param.17) | copy-start | bytes 3932164
Sparse Core Ops, SparseCore 0:
  1590.4 412.3 all-gather.2
  4260.9 411.7 all-gather.4
where the time goes:
time: 4750 us; the launch traced here: 4740 us
  waiting for transfers between devices  1830 us (39%)
  matrix products  1390 us (29%)
  blocking collectives  1040 us (22%)
  local copies, waits for them, and re-layouts  238 us (5%)
  other arithmetic  214 us (5%)
    all_to_all x1, blocking collectives, sum_partials(): received = lax.all_to_all(stacked, 'tp', 1, 1, tiled=True)  1040 us
    all_to_all x1, waiting for transfers between devices, sum_partials(): received = lax.all_to_all(stacked, 'tp', 1, 1, tiled=True)  1020 us
    all_gather x1, waiting for transfers between devices, layer_shard(): lax.all_gather(rms_norm(hidden_rows, mlp_gain), 'tp', axis=1, tiled=True)  413 us
    all_gather x1, waiting for transfers between devices, layer_shard(): y = lax.all_gather(out_rows, 'tp', axis=1, tiled=True)  405 us
    dot_general x1, matrix products, layer_shard(): jnp.einsum('bsf,fd->bsd', gated, w_down, preferred_element_type=jnp.float32)  372 us
    dot_general x1, matrix products, layer_shard(): jnp.einsum('bsd,df->bsf', normed_mlp, w_up, preferred_element_type=jnp.fl...  357 us
    dot_general x1, matrix products, layer_shard(): jnp.einsum('bsd,df->bsf', normed_mlp, w_gate, preferred_element_type=jnp....  357 us
    reshape x2, local copies, waits for them, and re-layouts, sum_partials(): partial.reshape(batch_size, tp_size, seq_len // tp_size, model_width)  122 us
  transfers between devices with their start and end apart: 3, of which 3 were waited for; matrix products, arithmetic and copies ran while one was open for 0% of the time, Pallas kernels for 0%

commit v1 on v0

v1 whole, which is shorter than its diff:
```python
import functools

import jax
import jax.numpy as jnp
from jax import lax
from jax.experimental import pallas as pl
from jax.experimental.pallas import tpu as pltpu
from jax.sharding import PartitionSpec as P


EPS = 1e-5
ROPE_BASE = 10000.0
CHUNKS = (6, 6, 6, 4, 2)
SETTLED = 2
Q_BLOCK = 128
COL_TILE = 512


def norm_rows(src_ref, dst_ref, gain_ref, rows, step):
    gain = gain_ref[...].astype(jnp.float32)

    def body(index, carry):
        part = pl.ds(pl.multiple_of(index * step, step), step)
        rows32 = src_ref[part, :].astype(jnp.float32)
        inv_rms = lax.rsqrt(jnp.mean(rows32 * rows32, axis=-1, keepdims=True) + EPS)
        dst_ref[part, :] = (rows32 * inv_rms * gain).astype(jnp.bfloat16)
        return carry

    lax.fori_loop(0, rows // step, body, 0)


def attend_kernel(first, lens_ref, x_ref, wq_ref, wkv_ref, gain_ref, cos_ref, sin_ref, o_ref, k_ref, v_ref, normed_ref):
    seq_len = x_ref.shape[0]
    head_dim = cos_ref.shape[1]
    group_size = wq_ref.shape[1] // head_dim
    length = lens_ref[first + pl.program_id(0)]
    norm_rows(x_ref, normed_ref, gain_ref, seq_len, 16)
    normed = normed_ref[...]
    kv_pre = jnp.dot(normed, wkv_ref[...], preferred_element_type=jnp.float32)
    q_pre = jnp.dot(normed, wq_ref[...], preferred_element_type=jnp.float32)
    cos_tab = cos_ref[...]
    sin_tab = sin_ref[...]
    even_lane = lax.broadcasted_iota(jnp.int32, (seq_len, head_dim), 1) % 2 == 0

    def rotate(vecs):
        swapped = jnp.where(even_lane, pltpu.roll(vecs, head_dim - 1, 1), pltpu.roll(vecs, 1, 1))
        return (vecs * cos_tab + swapped * sin_tab).astype(jnp.bfloat16)

    valid = lax.broadcasted_iota(jnp.int32, (seq_len, head_dim), 0) < length
    keys32 = jnp.where(valid, rotate(kv_pre[:, :head_dim]).astype(jnp.float32), 0.0)
    values32 = jnp.where(valid, kv_pre[:, head_dim:], 0.0)
    keys = keys32.astype(jnp.bfloat16)
    values = values32.astype(jnp.bfloat16)
    k_ref[...] = keys
    v_ref[...] = values
    queries = [rotate(q_pre[:, j * head_dim:(j + 1) * head_dim]) for j in range(group_size)]
    for block in range(seq_len // Q_BLOCK):
        lo, hi = block * Q_BLOCK, (block + 1) * Q_BLOCK
        t_pos = lo + lax.broadcasted_iota(jnp.int32, (Q_BLOCK, hi), 0)
        u_pos = lax.broadcasted_iota(jnp.int32, (Q_BLOCK, hi), 1)
        allowed = (u_pos <= t_pos) & (u_pos < length)
        for j in range(group_size):
            scores = lax.dot_general(queries[j][lo:hi], keys[:hi], (((1,), (1,)), ((), ())), preferred_element_type=jnp.float32) * head_dim ** -0.5
            scores = jnp.where(allowed, scores, -jnp.inf)
            expd = jnp.exp(scores - jnp.max(scores, axis=-1, keepdims=True))
            probs = (expd / jnp.sum(expd, axis=-1, keepdims=True)).astype(jnp.bfloat16)
            o_ref[lo:hi, j * head_dim:(j + 1) * head_dim] = jnp.dot(probs, values[:hi], preferred_element_type=jnp.float32).astype(jnp.bfloat16)


def attend(first, count, x, seq_lens, w_query, w_kv, gain, cos_tab, sin_tab):
    _, seq_len, width = x.shape
    q_cols = w_query.shape[1]
    head_dim = cos_tab.shape[1]
    whole = lambda *shape: pl.BlockSpec(shape, lambda b, lens: (0,) * len(shape))
    per_seq = lambda cols: pl.BlockSpec((None, seq_len, cols), lambda b, lens: (b, 0, 0))
    grid_spec = pltpu.PrefetchScalarGridSpec(
        num_scalar_prefetch=1,
        grid=(count,),
        in_specs=[
            pl.BlockSpec((None, seq_len, width), lambda b, lens: (first + b, 0, 0)),
            whole(width, q_cols),
            whole(width, 2 * head_dim),
            whole(1, width),
            whole(seq_len, head_dim),
            whole(seq_len, head_dim),
        ],
        out_specs=[per_seq(q_cols), per_seq(head_dim), per_seq(head_dim)],
        scratch_shapes=[pltpu.VMEM((seq_len, width), jnp.bfloat16)],
    )
    return pl.pallas_call(
        functools.partial(attend_kernel, first),
        grid_spec=grid_spec,
        out_shape=[jax.ShapeDtypeStruct((count, seq_len, cols), jnp.bfloat16) for cols in (q_cols, head_dim, head_dim)],
        compiler_params=pltpu.CompilerParams(vmem_limit_bytes=56 * 1024 * 1024),
        cost_estimate=pl.CostEstimate(flops=2 * count * seq_len * width * (q_cols + 2 * head_dim), bytes_accessed=2 * count * seq_len * (width + q_cols), transcendentals=0),
        name="attend",
    )(seq_lens, x, w_query, w_kv, gain, cos_tab, sin_tab)


def project_kernel(o_ref, w_ref, x_ref, gain_ref, h_ref, n_ref):
    groups, rows, depth = o_ref.shape
    tile = w_ref.shape[1]
    columns = pl.ds(pl.multiple_of(pl.program_id(0) * tile, tile), tile)
    total = jnp.zeros((rows, tile), jnp.float32)
    for index in range(groups):
        partial = jnp.dot(o_ref[index], w_ref[index * depth:(index + 1) * depth, :], preferred_element_type=jnp.float32)
        total = total + partial.astype(jnp.bfloat16).astype(jnp.float32)
    h_ref[:, columns] = (x_ref[...].astype(jnp.float32) + total).astype(jnp.bfloat16)

    @pl.when(pl.program_id(0) == pl.num_programs(0) - 1)
    def _():
        norm_rows(h_ref, n_ref, gain_ref, rows, 16)


def project(o_all, w_out_all, x_rows, gain):
    groups, rows, depth = o_all.shape
    width = w_out_all.shape[1]
    out = jax.ShapeDtypeStruct((rows, width), jnp.bfloat16)
    return pl.pallas_call(
        project_kernel,
        grid=(width // COL_TILE,),
        in_specs=[
            pl.BlockSpec((groups, rows, depth), lambda j: (0, 0, 0)),
            pl.BlockSpec((groups * depth, COL_TILE), lambda j: (0, j)),
            pl.BlockSpec((rows, COL_TILE), lambda j: (0, j)),
            pl.BlockSpec((1, width), lambda j: (0, 0)),
        ],
        out_specs=[pl.BlockSpec((rows, width), lambda j: (0, 0))] * 2,
        out_shape=[out, out],
        compiler_params=pltpu.CompilerParams(vmem_limit_bytes=48 * 1024 * 1024),
        cost_estimate=pl.CostEstimate(flops=2 * rows * groups * depth * width, bytes_accessed=2 * (groups * depth * width + 4 * rows * width), transcendentals=0),
        name="project",
    )(o_all, w_out_all, x_rows, gain)


def solution(mesh):
    tp_size = mesh.shape["tp"]
    last = len(CHUNKS) - 1

    def swap(value, bit):
        return lax.ppermute(value, "tp", [(index, index ^ bit) for index in range(tp_size)])

    def sum_partials(partial, resid_rows):
        rows, width = resid_rows.shape
        half = rows // 2
        me = lax.axis_index("tp")
        core, chip = me % 2, me // 2
        blocks = partial.reshape(tp_size // 2, 2, rows, width)
        take = lambda which: lax.dynamic_index_in_dim(blocks, which, 1, keepdims=False)
        ours = take(core)
        theirs = swap(take(1 - core), 1)

        def both(step, lo):
            pick = lambda value: lax.dynamic_slice(value, (chip ^ step, lo, 0), (1, half, width))[0].astype(jnp.float32)
            return pick(ours) + pick(theirs)

        x_far, y_far = swap(both(3, 0), 2), swap(both(3, half), 4)
        x_near, y_near = swap(both(1, 0), 2), swap(both(2, half), 4)
        x_late = swap(both(1, half) + y_far, 2)
        y_late = swap(both(2, 0) + x_far, 4)
        upper = resid_rows[:half].astype(jnp.float32) + (both(0, 0) + x_near + y_late)
        lower = resid_rows[half:].astype(jnp.float32) + (both(0, half) + x_late + y_near)
        return jnp.concatenate([upper.astype(jnp.bfloat16), lower.astype(jnp.bfloat16)], axis=0)

    def layer_shard(x, seq_lens, w_query, w_key, w_value, w_out, w_gate, w_up, w_down, attn_gain, mlp_gain, k_cache, v_cache):
        batch_size, seq_len, width = x.shape
        head_dim = k_cache.shape[3]
        tp_index = lax.axis_index("tp")
        w_out_all = lax.all_gather(w_out, "tp", axis=0, tiled=True)
        w_kv = jnp.concatenate([w_key, w_value], axis=1)
        inv_freq = ROPE_BASE ** (-jnp.arange(0, head_dim, 2).astype(jnp.float32) / head_dim)
        angles = jnp.repeat(jnp.arange(seq_len).astype(jnp.float32)[:, None] * inv_freq[None, :], 2, axis=1)
        sign = jnp.where(jnp.arange(head_dim) % 2 == 0, -1.0, 1.0)
        cos_tab = jnp.cos(angles)
        sin_tab = jnp.sin(angles) * sign
        x_flat = x.reshape(batch_size * seq_len, width)
        y = jnp.zeros((batch_size * seq_len, width), jnp.bfloat16)
        gathered = []
        starts = [sum(CHUNKS[:index]) for index in range(len(CHUNKS))]
        attended, received = [], []
        for first, count in zip(starts, CHUNKS):
            attended.append(attend(first, count, x, seq_lens, w_query, w_kv, attn_gain[None], cos_tab, sin_tab))
            received.append(lax.all_to_all(attended[-1][0].reshape(tp_size, count * seq_len // tp_size, -1), "tp", 0, 0, tiled=True))
        new_keys = [keys for _, keys, _ in attended]
        new_values = [values for _, _, values in attended]
        w_out_all, new_keys = lax.optimization_barrier((w_out_all, new_keys))
        for index, (first, count) in enumerate(zip(starts, CHUNKS)):
            start_row = first * seq_len
            rows = count * seq_len // tp_size
            x_rows = lax.dynamic_slice_in_dim(x_flat, start_row + tp_index * rows, rows, axis=0)
            hidden, normed = project(received[index], w_out_all, x_rows, mlp_gain[None])
            normed_all = lax.all_gather(normed, "tp", axis=0, tiled=True)
            gate_pre = jnp.dot(normed_all, w_gate, preferred_element_type=jnp.float32)
            up_pre = jnp.dot(normed_all, w_up, preferred_element_type=jnp.float32)
            gated = (jax.nn.silu(gate_pre) * up_pre).astype(jnp.bfloat16)
            if index == last:
                gated, settled = lax.optimization_barrier((gated, gathered[:SETTLED]))
                for row, block in zip(starts, settled):
                    y = lax.dynamic_update_slice(y, block, (row * seq_len, 0))
                gated, y = lax.optimization_barrier((gated, y))
            mlp_part = jnp.dot(gated, w_down, preferred_element_type=jnp.float32).astype(jnp.bfloat16)
            out_rows = sum_partials(mlp_part, hidden)
            gathered.append(lax.all_gather(out_rows, "tp", axis=0, tiled=True))
        for index in range(SETTLED, len(CHUNKS)):
            y = lax.dynamic_update_slice(y, gathered[index], (starts[index] * seq_len, 0))
        k_cache_out = lax.dynamic_update_slice(k_cache, jnp.concatenate(new_keys)[:, :, None, :], (0, 0, 0, 0))
        v_cache_out = lax.dynamic_update_slice(v_cache, jnp.concatenate(new_values)[:, :, None, :], (0, 0, 0, 0))
        return y.reshape(x.shape), k_cache_out, v_cache_out

    cache_spec = P("dp", None, "tp", None)
    return jax.shard_map(layer_shard, mesh=mesh, in_specs=(P("dp", None, None), P("dp"), P(None, "tp"), P(None, "tp"), P(None, "tp"), P("tp", None), P(None, "tp"), P(None, "tp"), P("tp", None), P(), P(), cache_spec, cache_spec), out_specs=(P("dp", None, None), cache_spec, cache_spec), check_vma=False)
```

time: 4750 us -> 2760 us (0.58)
  waiting for transfers between devices: 1830 us -> 627 us
  blocking collectives: 1040 us -> 133 us
  Pallas kernels: 0 us -> 473 us
  matrix products: 1390 us -> 1200 us
  other arithmetic: 214 us -> 89 us
  local copies, waits for them, and re-layouts: 238 us -> 173 us
    all_to_all x1 -> x3, waiting for transfers between devices: 1020 us -> 27.9 us  [layer_shard(): lax.all_to_all(attended[-1][0].reshape(tp_size, count * seq_len // tp_siz...]
    all_to_all x1 -> x2, blocking collectives: 1040 us -> 133 us  [layer_shard(): lax.all_to_all(attended[-1][0].reshape(tp_size, count * seq_len // tp_siz...]
    all_gather x2 -> x11, waiting for transfers between devices: 818 us -> 8.81 us  [the longest x5 8.75 us: layer_shard(): gathered.append(lax.all_gather(out_rows, 'tp', axis=0, tiled=True))]
    ppermute x0 -> x35, waiting for transfers between devices: none -> 590 us  [swap(): lax.ppermute(value, 'tp', [(index, index ^ bit) for index in range(tp_siz...]
    pallas_call x0 -> x10, Pallas kernels: none -> 473 us  [the longest x5 329 us: attend(): pl.pallas_call(functools.partial(attend_kernel, first), grid_spec=grid_sp...]
    dot_general x9 -> x15, matrix products: 1390 us -> 1200 us  [the longest x5 421 us: layer_shard(): up_pre = jnp.dot(normed_all, w_up, preferred_element_type=jnp.float32)]
    reduce_sum x5 -> x0, other arithmetic: 172 us -> none  [the longest x2 111 us: sum_partials(): summed = jnp.sum(received.astype(jnp.float32), axis=1)]
    reshape x2 -> x0, local copies, waits for them, and re-layouts: 122 us -> none  [sum_partials(): partial.reshape(batch_size, tp_size, seq_len // tp_size, model_width)]
  transfers between devices with their start and end apart: 3 -> 49, of which waited for: 3 -> 23; matrix products, arithmetic and copies ran while one was open for 0% -> 52% of each run, Pallas kernels for 0% -> 16%
where the time goes in v1:
time: 2760 us; the launch traced here: 2750 us
  matrix products  1200 us (43%)
  waiting for transfers between devices  627 us (23%)
  Pallas kernels  473 us (17%)
  local copies, waits for them, and re-layouts  173 us (6%)
  blocking collectives  133 us (5%)
  other arithmetic  89 us (3%)
  starting transfers between devices  42.6 us (2%)
    ppermute x35, waiting for transfers between devices, swap(): lax.ppermute(value, 'tp', [(index, index ^ bit) for index in range(tp_siz...  590 us
    dot_general x5, matrix products, layer_shard(): up_pre = jnp.dot(normed_all, w_up, preferred_element_type=jnp.float32)  421 us
    dot_general x5, matrix products, layer_shard(): gate_pre = jnp.dot(normed_all, w_gate, preferred_element_type=jnp.float32)  396 us
    dot_general x5, matrix products, layer_shard(): jnp.dot(gated, w_down, preferred_element_type=jnp.float32)  381 us
    pallas_call x5, Pallas kernels, attend(): pl.pallas_call(functools.partial(attend_kernel, first), grid_spec=grid_sp...  329 us
    pallas_call x5, Pallas kernels, project(): pl.pallas_call(project_kernel, grid=(width // COL_TILE,), in_specs=[pl.Bl...  143 us
    all_to_all x2, blocking collectives, layer_shard(): lax.all_to_all(attended[-1][0].reshape(tp_size, count * seq_len // tp_siz...  133 us
    dynamic_update_slice x2, local copies, waits for them, and re-layouts, layer_shard(): y = lax.dynamic_update_slice(y, block, (row * seq_len, 0))  57.1 us
  transfers between devices with their start and end apart: 49, of which 23 were waited for; matrix products, arithmetic and copies ran while one was open for 52% of the time, Pallas kernels for 16%

profile of v1, /device:TPU:0, one launch (start us, length us, event | category | flops | bytes accessed | tf_op | source)
XLA Modules:
  0.0 2749.5 jit_solution(2054169418391031232)
XLA Ops:
  20.4 83.3 %attend.6 = (bf16[6,384,640]{2,1,0:T(8,128)(2,1)}, bf16[6,384,128]{2,1,0:T(8,128)(2,1)}, bf16[6,384,128]{2,1,0:T(8,128)(2,1)}) custom-call(s32[24]{0:T(128)} %lens_ref.9, bf16[24,384,5120]{2,1,0:T(8,128)(2,1)} %x_ref.9, bf16[5120,640]{1,0:T(8,128)(2,1)} %wq_ref.9, bf16[5120,256]{1,0:T(8,128)(2,1)} %copy-done.11, bf16[1,5120]{1,0:T(2,128)(2,1)} %broadcast_in_dim.53.gain_ref, ...), custom_call_target="tpu_custom_call" | custom-call | flops 21139292160 | bytes 26542080 | tf_op jit(solution)/shard_map/attend/pallas_call | solution.py:90
  108.3 10.3 constant_dynamic-slice_fusion
  118.6 55.2 %attend.9 = (bf16[4,384,640]{2,1,0:T(8,128)(2,1)}, bf16[4,384,128]{2,1,0:T(8,128)(2,1)}, bf16[4,384,128]{2,1,0:T(8,128)(2,1)}) custom-call(s32[24]{0:T(128)} %lens_ref.9, bf16[24,384,5120]{2,1,0:T(8,128)(2,1)} %x_ref.9, bf16[5120,640]{1,0:T(8,128)(2,1)} %wq_ref.9, bf16[5120,256]{1,0:T(8,128)(2,1)} %copy-done.11, bf16[1,5120]{1,0:T(2,128)(2,1)} %broadcast_in_dim.53.gain_ref, ...), custom_call_target="tpu_custom_call" | custom-call | flops 14092861440 | bytes 17694720 | tf_op jit(solution)/shard_map/attend/pallas_call | solution.py:90
  173.8 80.3 %attend.8 = (bf16[6,384,640]{2,1,0:T(8,128)(2,1)}, bf16[6,384,128]{2,1,0:T(8,128)(2,1)}, bf16[6,384,128]{2,1,0:T(8,128)(2,1)}) custom-call(s32[24]{0:T(128)} %lens_ref.9, bf16[24,384,5120]{2,1,0:T(8,128)(2,1)} %x_ref.9, bf16[5120,640]{1,0:T(8,128)(2,1)} %wq_ref.9, bf16[5120,256]{1,0:T(8,128)(2,1)} %copy-done.11, bf16[1,5120]{1,0:T(2,128)(2,1)} %broadcast_in_dim.53.gain_ref, ...), custom_call_target="tpu_custom_call" | custom-call | flops 21139292160 | bytes 26542080 | tf_op jit(solution)/shard_map/attend/pallas_call | solution.py:90
  254.1 30.9 %attend.5 = (bf16[2,384,640]{2,1,0:T(8,128)(2,1)}, bf16[2,384,128]{2,1,0:T(8,128)(2,1)}, bf16[2,384,128]{2,1,0:T(8,128)(2,1)}) custom-call(s32[24]{0:T(128)} %lens_ref.9, bf16[24,384,5120]{2,1,0:T(8,128)(2,1)} %x_ref.9, bf16[5120,640]{1,0:T(8,128)(2,1)} %wq_ref.9, bf16[5120,256]{1,0:T(8,128)(2,1)} %copy-done.11, bf16[1,5120]{1,0:T(2,128)(2,1)} %broadcast_in_dim.53.gain_ref, ...), custom_call_target="tpu_custom_call" | custom-call | flops 7046430720 | bytes 8847360 | tf_op jit(solution)/shard_map/attend/pallas_call | solution.py:90
  285.0 79.7 %attend.7 = (bf16[6,384,640]{2,1,0:T(8,128)(2,1)}, bf16[6,384,128]{2,1,0:T(8,128)(2,1)}, bf16[6,384,128]{2,1,0:T(8,128)(2,1)}) custom-call(s32[24]{0:T(128)} %lens_ref.9, bf16[24,384,5120]{2,1,0:T(8,128)(2,1)} %x_ref.9, bf16[5120,640]{1,0:T(8,128)(2,1)} %wq_ref.9, bf16[5120,256]{1,0:T(8,128)(2,1)} %copy-done.11, bf16[1,5120]{1,0:T(2,128)(2,1)} %broadcast_in_dim.53.gain_ref, ...), custom_call_target="tpu_custom_call" | custom-call | flops 21139292160 | bytes 26542080 | tf_op jit(solution)/shard_map/attend/pallas_call | solution.py:90
  366.3 30.9 %project.6 = (bf16[288,5120]{1,0:T(8,128)(2,1)S(1)}, bf16[288,5120]{1,0:T(8,128)(2,1)}) custom-call(bf16[8,288,640]{2,1,0:T(8,128)(2,1)} %copy-done.12, bf16[5120,5120]{1,0:T(8,128)(2,1)} %all-gather.12.cloned.1.call-done.w_ref, bf16[288,5120]{1,0:T(8,128)(2,1)} %get-tuple-element.77.x_ref, bf16[1,5120]{1,0:T(2,128)(2,1)S(1)} %broadcast_in_dim.58.gain_ref), custom_call_target="tpu_custom_call" | custom-call | flops 15099494400 | bytes 64225280 | tf_op jit(solution)/shard_map/project/pallas_call | solution.py:119
  400.6 66.3 %all_to_all.25.o_ref = bf16[8,288,640]{2,1,0:T(8,128)(2,1)} all-to-all(bf16[8,288,640]{2,1,0:T(8,128)(2,1)S(1)} %bitcast.326), channel_id=1, replica_groups=mesh['dp'=1,'tp'=8] {'tp'}, dimensions={0} | all-to-all | bytes 5898240 | tf_op jit(solution)/shard_map/all_to_all | solution.py:183
  466.9 33.1 %project.7 = (bf16[288,5120]{1,0:T(8,128)(2,1)S(1)}, bf16[288,5120]{1,0:T(8,128)(2,1)}) custom-call(bf16[8,288,640]{2,1,0:T(8,128)(2,1)} %all_to_all.25.o_ref, bf16[5120,5120]{1,0:T(8,128)(2,1)} %all-gather.12.cloned.1.call-done.w_ref, bf16[288,5120]{1,0:T(8,128)(2,1)} %get-tuple-element.76.x_ref, bf16[1,5120]{1,0:T(2,128)(2,1)S(1)} %broadcast_in_dim.58.gain_ref), custom_call_target="tpu_custom_call" | custom-call | flops 15099494400 | bytes 64225280 | tf_op jit(solution)/shard_map/project/pallas_call | solution.py:119
  503.4 66.4 %all_to_all.26.o_ref = bf16[8,288,640]{2,1,0:T(8,128)(2,1)} all-to-all(bf16[8,288,640]{2,1,0:T(8,128)(2,1)S(1)} %bitcast.325), channel_id=1, replica_groups=mesh['dp'=1,'tp'=8] {'tp'}, dimensions={0} | all-to-all | bytes 5898240 | tf_op jit(solution)/shard_map/all_to_all | solution.py:183
  569.8 32.4 %project.8 = (bf16[288,5120]{1,0:T(8,128)(2,1)S(1)}, bf16[288,5120]{1,0:T(8,128)(2,1)}) custom-call(bf16[8,288,640]{2,1,0:T(8,128)(2,1)} %all_to_all.26.o_ref, bf16[5120,5120]{1,0:T(8,128)(2,1)} %all-gather.12.cloned.1.call-done.w_ref, bf16[288,5120]{1,0:T(8,128)(2,1)} %get-tuple-element.75.x_ref, bf16[1,5120]{1,0:T(2,128)(2,1)S(1)} %broadcast_in_dim.58.gain_ref), custom_call_target="tpu_custom_call" | custom-call | flops 15099494400 | bytes 64225280 | tf_op jit(solution)/shard_map/project/pallas_call | solution.py:119
  609.2 27.9 %all-to-all-done.4.o_ref = bf16[8,192,640]{2,1,0:T(8,128)(2,1)S(1)} async-done(((bf16[8,192,640]{2,1,0:T(8,128)(2,1)}), bf16[8,192,640]{2,1,0:T(8,128)(2,1)S(1)}, u32[]{:S(2)}, u32[]{:S(2)}) %all-to-all-start.4) | async-done | bytes 1966112 | tf_op jit(solution)/shard_map/all_to_all | solution.py:183
  640.2 24.2 project.9
  667.2 97.6 %fusion.51 = f32[2304,3456]{1,0:T(8,128)} fusion(bf16[2304,5120]{1,0:T(8,128)(2,1)} %all-gather.16.cloned.1.call-done, bf16[5120,3456]{1,0:T(8,128)(2,1)} %param.19), kind=kOutput, calls=%fused_computation.141 | convolution fusion | flops 81537269760 | bytes 90832896 | tf_op jit(solution)/shard_map/dot_general | solution.py:193
  764.8 104.8 %multiply_convert_fusion.2 = bf16[2304,3456]{1,0:T(8,128)(2,1)} fusion(f32[2304,3456]{1,0:T(8,128)} %fusion.51, bf16[2304,5120]{1,0:T(8,128)(2,1)} %all-gather.16.cloned.1.call-done, bf16[5120,3456]{1,0:T(8,128)(2,1)} %param.20), kind=kOutput, calls=%fused_computation.2 | convolution fusion | flops 81585045504 | bytes 106758144 | tf_op jit(solution)/shard_map/dot_general | solution.py:194
  869.7 94.9 %convolution_convert_fusion.2 = bf16[2304,5120]{1,0:T(8,128)(2,1)} fusion(bf16[2304,3456]{1,0:T(8,128)(2,1)} %multiply_convert_fusion.2, bf16[3456,5120]{1,0:T(8,128)(2,1)} %param.21), kind=kOutput, calls=%fused_computation.5 | convolution fusion | flops 81549066240 | bytes 74907648 | tf_op jit(solution)/shard_map/dot_general | solution.py:201
  974.9 97.1 %fusion.52 = f32[2304,3456]{1,0:T(8,128)} fusion(bf16[2304,5120]{1,0:T(8,128)(2,1)} %all-gather.20.cloned.1.call-done, bf16[5120,3456]{1,0:T(8,128)(2,1)} %param.19), kind=kOutput, calls=%fused_computation.142 | convolution fusion | flops 81537269760 | bytes 90832896 | tf_op jit(solution)/shard_map/dot_general | solution.py:193
  1071.9 104.7 %multiply_convert_fusion.1 = bf16[2304,3456]{1,0:T(8,128)(2,1)} fusion(f32[2304,3456]{1,0:T(8,128)} %fusion.52, bf16[2304,5120]{1,0:T(8,128)(2,1)} %all-gather.20.cloned.1.call-done, bf16[5120,3456]{1,0:T(8,128)(2,1)} %param.20), kind=kOutput, calls=%fused_computation.1 | convolution fusion | flops 81585045504 | bytes 106758144 | tf_op jit(solution)/shard_map/dot_general | solution.py:194
  1176.7 94.8 %convolution_convert_fusion.1 = bf16[2304,5120]{1,0:T(8,128)(2,1)} fusion(bf16[2304,3456]{1,0:T(8,128)(2,1)} %multiply_convert_fusion.1, bf16[3456,5120]{1,0:T(8,128)(2,1)} %param.21), kind=kOutput, calls=%fused_computation.4 | convolution fusion | flops 81549066240 | bytes 74907648 | tf_op jit(solution)/shard_map/dot_general | solution.py:201
  1271.5 10.0 dynamic-slice_bitcast_fusion.1
  1282.9 22.5 project.5
  1319.8 91.3 %collective-permute-done.4 = f32[144,5120]{1,0:T(8,128)S(1)} collective-permute-done((f32[144,5120]{1,0:T(8,128)}, f32[144,5120]{1,0:T(8,128)S(1)}, u32[]{:S(2)}, u32[]{:S(2)}) %collective-permute-start.4) | collective-permute-done | bytes 2949152 | tf_op jit(solution)/shard_map/ppermute | solution.py:141
  1430.9 42.9 %collective-permute-done.1 = f32[144,5120]{1,0:T(8,128)S(1)} collective-permute-done((f32[144,5120]{1,0:T(8,128)}, f32[144,5120]{1,0:T(8,128)S(1)}, u32[]{:S(2)}, u32[]{:S(2)}) %collective-permute-start.1) | collective-permute-done | bytes 2949152 | tf_op jit(solution)/shard_map/ppermute | solution.py:141
  1474.3 63.2 %collective-permute-done.3 = f32[144,5120]{1,0:T(8,128)} collective-permute-done((f32[144,5120]{1,0:T(8,128)}, f32[144,5120]{1,0:T(8,128)}, u32[]{:S(2)}, u32[]{:S(2)}) %collective-permute-start.3) | collective-permute-done | bytes 2949152 | tf_op jit(solution)/shard_map/ppermute | solution.py:141
  1546.1 99.2 %fusion.53 = f32[2304,3456]{1,0:T(8,128)} fusion(bf16[2304,5120]{1,0:T(8,128)(2,1)} %all-gather.24.cloned.1.call-done, bf16[5120,3456]{1,0:T(8,128)(2,1)} %param.19), kind=kOutput, calls=%fused_computation.143 | convolution fusion | flops 81537269760 | bytes 90832896 | tf_op jit(solution)/shard_map/dot_general | solution.py:193
  1658.0 105.0 %multiply_convert_fusion = bf16[2304,3456]{1,0:T(8,128)(2,1)} fusion(f32[2304,3456]{1,0:T(8,128)} %fusion.53, bf16[2304,5120]{1,0:T(8,128)(2,1)} %all-gather.24.cloned.1.call-done, bf16[5120,3456]{1,0:T(8,128)(2,1)} %param.20), kind=kOutput, calls=%fused_computation | convolution fusion | flops 81585045504 | bytes 106758144 | tf_op jit(solution)/shard_map/dot_general | solution.py:194
  1763.0 58.7 %collective-permute-done.10 = f32[144,5120]{1,0:T(8,128)} collective-permute-done((f32[144,5120]{1,0:T(8,128)}, f32[144,5120]{1,0:T(8,128)}, u32[]{:S(2)}, u32[]{:S(2)}) %collective-permute-start.10) | collective-permute-done | bytes 2949152 | tf_op jit(solution)/shard_map/ppermute | solution.py:141
  1831.1 96.0 %convolution_convert_fusion = bf16[2304,5120]{1,0:T(8,128)(2,1)} fusion(bf16[2304,3456]{1,0:T(8,128)(2,1)} %multiply_convert_fusion, bf16[3456,5120]{1,0:T(8,128)(2,1)} %param.21), kind=kOutput, calls=%fused_computation.3 | convolution fusion | flops 81549066240 | bytes 74907648 | tf_op jit(solution)/shard_map/dot_general | solution.py:201
  1933.3 19.9 collective-permute-done.14
  1966.1 62.7 %collective-permute-done.18 = f32[144,5120]{1,0:T(8,128)S(1)} collective-permute-done((f32[144,5120]{1,0:T(8,128)S(1)}, f32[144,5120]{1,0:T(8,128)S(1)}, u32[]{:S(2)}, u32[]{:S(2)}) %collective-permute-start.18) | collective-permute-done | bytes 2949152 | tf_op jit(solution)/shard_map/ppermute | solution.py:141
  2038.7 67.4 %fusion.54 = f32[1536,3456]{1,0:T(8,128)} fusion(bf16[1536,5120]{1,0:T(8,128)(2,1)} %all-gather.28.cloned.1.call-done, bf16[5120,3456]{1,0:T(8,128)(2,1)} %param.19), kind=kOutput, calls=%fused_computation.144 | convolution fusion | flops 54358179840 | bytes 72351744 | tf_op jit(solution)/shard_map/dot_general | solution.py:193
  2106.1 48.6 %collective-permute-done.17 = f32[144,5120]{1,0:T(8,128)} collective-permute-done((f32[144,5120]{1,0:T(8,128)}, f32[144,5120]{1,0:T(8,128)}, u32[]{:S(2)}, u32[]{:S(2)}) %collective-permute-start.17) | collective-permute-done | bytes 2949152 | tf_op jit(solution)/shard_map/ppermute | solution.py:141
  2163.6 72.4 %multiply_convert_fusion.3 = bf16[1536,3456]{1,0:T(8,128)(2,1)S(1)} fusion(f32[1536,3456]{1,0:T(8,128)} %fusion.54, bf16[1536,5120]{1,0:T(8,128)(2,1)} %all-gather.28.cloned.1.call-done, bf16[5120,3456]{1,0:T(8,128)(2,1)} %param.20), kind=kOutput, calls=%fused_computation.6 | convolution fusion | flops 54390030336 | bytes 82968576 | tf_op jit(solution)/shard_map/dot_general | solution.py:194
  2236.0 63.0 %convolution_convert_fusion.3 = bf16[1536,5120]{1,0:T(8,128)(2,1)} fusion(bf16[1536,3456]{1,0:T(8,128)(2,1)S(1)} %multiply_convert_fusion.3, bf16[3456,5120]{1,0:T(8,128)(2,1)} %param.21), kind=kOutput, calls=%fused_computation.7 | convolution fusion | flops 54366044160 | bytes 61734912 | tf_op jit(solution)/shard_map/dot_general | solution.py:201
  2302.8 12.4 collective-permute-done.21
  2322.7 41.6 %collective-permute-done.25 = f32[96,5120]{1,0:T(8,128)S(1)} collective-permute-done((f32[96,5120]{1,0:T(8,128)S(1)}, f32[96,5120]{1,0:T(8,128)S(1)}, u32[]{:S(2)}, u32[]{:S(2)}) %collective-permute-start.25) | collective-permute-done | bytes 1966112 | tf_op jit(solution)/shard_map/ppermute | solution.py:141
  2369.8 38.5 %collective-permute-done.22 = f32[96,5120]{1,0:T(8,128)S(1)} collective-permute-done((f32[96,5120]{1,0:T(8,128)S(1)}, f32[96,5120]{1,0:T(8,128)S(1)}, u32[]{:S(2)}, u32[]{:S(2)}) %collective-permute-start.22) | collective-permute-done | bytes 1966112 | tf_op jit(solution)/shard_map/ppermute | solution.py:141
  2408.2 39.6 %collective-permute-done.24 = f32[96,5120]{1,0:T(8,128)S(1)} collective-permute-done((f32[96,5120]{1,0:T(8,128)S(1)}, f32[96,5120]{1,0:T(8,128)S(1)}, u32[]{:S(2)}, u32[]{:S(2)}) %collective-permute-start.24) | collective-permute-done | bytes 1966112 | tf_op jit(solution)/shard_map/ppermute | solution.py:141
  2453.7 34.2 %fusion.50 = f32[768,3456]{1,0:T(8,128)S(1)} fusion(bf16[768,5120]{1,0:T(8,128)(2,1)} %all-gather.14.cloned.1.call-done, bf16[5120,3456]{1,0:T(8,128)(2,1)} %param.19), kind=kOutput, calls=%fused_computation.140 | convolution fusion | flops 27179089920 | bytes 53870592 | tf_op jit(solution)/shard_map/dot_general | solution.py:193
  2488.0 34.5 %multiply_convert_fusion.4 = bf16[768,3456]{1,0:T(8,128)(2,1)} fusion(f32[768,3456]{1,0:T(8,128)S(1)} %fusion.50, bf16[768,5120]{1,0:T(8,128)(2,1)S(1)} %copy-done.30, bf16[5120,3456]{1,0:T(8,128)(2,1)} %param.20), kind=kOutput, calls=%fused_computation.11 | convolution fusion | flops 27195015168 | bytes 59179008 | tf_op jit(solution)/shard_map/dot_general | solution.py:194
  2522.5 37.1 %dynamic_update_slice.21 = bf16[9216,5120]{1,0:T(8,128)(2,1)} pad(bf16[2304,5120]{1,0:T(8,128)(2,1)} %all-gather.18.cloned.1.call-done, bf16[]{:T(256)} %constant.1048.clone.1), padding=0_6912x0_0 | pad | bytes 117964800 | tf_op jit(solution)/shard_map/dynamic_update_slice | solution.py:199
  2559.5 20.0 constant_dynamic-update-slice_fusion.14
  2579.5 32.6 %convolution_convert_fusion.4 = bf16[768,5120]{1,0:T(8,128)(2,1)S(1)} fusion(bf16[768,3456]{1,0:T(8,128)(2,1)S(1)} %copy-done.31, bf16[3456,5120]{1,0:T(8,128)(2,1)} %param.21), kind=kOutput, calls=%fused_computation.12 | convolution fusion | flops 27183022080 | bytes 48562176 | tf_op jit(solution)/shard_map/dot_general | solution.py:201
  2623.7 20.6 collective-permute-done.32
  2648.6 18.1 collective-permute-done.29
  2666.8 18.9 collective-permute-done.31
  2693.3 20.3 constant_dynamic-update-slice_fusion.12
  2713.6 13.2 constant_dynamic-update-slice_fusion.15
  (213 shorter events, 215.4 us)
Async XLA Ops:
  7.2 357.5 %all-gather.12.cloned.1.call-start = ((), (), s32[]{:S(2)}) async-start(), calls=%async_computation.5 | async-start | bytes 58982400 | tf_op jit(solution)/shard_map/all_gather | solution.py:169
  103.7 261.0 %all-to-all-start.1 = ((bf16[8,288,640]{2,1,0:T(8,128)(2,1)}), bf16[8,288,640]{2,1,0:T(8,128)(2,1)S(1)}, u32[]{:S(2)}, u32[]{:S(2)}) async-start(bf16[8,288,640]{2,1,0:T(8,128)(2,1)} %bitcast.324), calls=%async_computation.1 | async-start | bytes 5898240 | tf_op jit(solution)/shard_map/all_to_all | solution.py:183
  107.7 559.5 %all-gather.16.cloned.1.call-start = ((), (), s32[]{:S(2)}) async-start(), calls=%async_computation.7 | async-start | bytes 26542080 | tf_op jit(solution)/shard_map/all_gather | solution.py:192
  398.8 576.1 %all-gather.20.cloned.1.call-start = ((), (), s32[]{:S(2)}) async-start(), calls=%async_computation.9 | async-start | bytes 26542080 | tf_op jit(solution)/shard_map/all_gather | solution.py:192
  501.6 1044.5 %all-gather.24.cloned.1.call-start = ((), (), s32[]{:S(2)}) async-start(), calls=%async_computation.11 | async-start | bytes 26542080 | tf_op jit(solution)/shard_map/all_gather | solution.py:192
  603.9 33.2 %all-to-all-start.4 = ((bf16[8,192,640]{2,1,0:T(8,128)(2,1)}), bf16[8,192,640]{2,1,0:T(8,128)(2,1)S(1)}, u32[]{:S(2)}, u32[]{:S(2)}) async-start(bf16[8,192,640]{2,1,0:T(8,128)(2,1)} %bitcast.327), calls=%async_computation.4 | async-start | bytes 3932160 | tf_op jit(solution)/shard_map/all_to_all | solution.py:183
  637.1 645.8 %all-to-all-start = ((bf16[8,96,640]{2,1,0:T(8,128)(2,1)}), bf16[8,96,640]{2,1,0:T(8,128)(2,1)}, u32[]{:S(2)}, u32[]{:S(2)}) async-start(bf16[8,96,640]{2,1,0:T(8,128)(2,1)} %bitcast), calls=%async_computation | async-start | bytes 1966080 | tf_op jit(solution)/shard_map/all_to_all | solution.py:183
  640.2 1398.5 %all-gather.28.cloned.1.call-start = ((), (), s32[]{:S(2)}) async-start(), calls=%async_computation.13 | async-start | bytes 17694720 | tf_op jit(solution)/shard_map/all_gather | solution.py:192
  667.1 1786.6 %all-gather.14.cloned.1.call-start = ((), (), s32[]{:S(2)}) async-start(), calls=%async_computation.6 | async-start | bytes 8847360 | tf_op jit(solution)/shard_map/all_gather | solution.py:192
  974.5 332.3 %collective-permute-start = (bf16[4,288,5120]{2,1,0:T(8,128)(2,1)}, bf16[4,288,5120]{2,1,0:T(8,128)(2,1)}, u32[]{:S(2)}, u32[]{:S(2)}) collective-permute-start(bf16[4,288,5120]{2,1,0:T(8,128)(2,1)} %dynamic-slice_bitcast_fusion.2), channel_id=1, source_target_pairs={{0,1},{1,0},{2,3},{3,2},{4,5},{5,4},{6,7},{7,6}} | collective-permute-start | bytes 35389448 | tf_op jit(solution)/shard_map/ppermute | solution.py:141
  1281.5 138.1 %collective-permute-start.7 = (bf16[4,288,5120]{2,1,0:T(8,128)(2,1)}, bf16[4,288,5120]{2,1,0:T(8,128)(2,1)}, u32[]{:S(2)}, u32[]{:S(2)}) collective-permute-start(bf16[4,288,5120]{2,1,0:T(8,128)(2,1)} %dynamic-slice_bitcast_fusion.1), channel_id=1, source_target_pairs={{0,1},{1,0},{2,3},{3,2},{4,5},{5,4},{6,7},{7,6}} | collective-permute-start | bytes 35389448 | tf_op jit(solution)/shard_map/ppermute | solution.py:141
  1306.5 1216.0 %all-gather.18.cloned.1.call-start = ((), (), s32[]{:S(2)}) async-start(), calls=%async_computation.8 | async-start | bytes 26542080 | tf_op jit(solution)/shard_map/all_gather | solution.py:203
  1315.7 95.3 %collective-permute-start.4 = (f32[144,5120]{1,0:T(8,128)}, f32[144,5120]{1,0:T(8,128)S(1)}, u32[]{:S(2)}, u32[]{:S(2)}) collective-permute-start(f32[144,5120]{1,0:T(8,128)} %get-tuple-element.98), channel_id=1, source_target_pairs={{0,4},{1,5},{2,6},{3,7},{4,0},{5,1},{6,2},{7,3}} | collective-permute-start | bytes 8847368 | tf_op jit(solution)/shard_map/ppermute | solution.py:141
  1317.6 93.4 %collective-permute-start.2 = (f32[144,5120]{1,0:T(8,128)S(1)}, f32[144,5120]{1,0:T(8,128)S(1)}, u32[]{:S(2)}, u32[]{:S(2)}) collective-permute-start(f32[144,5120]{1,0:T(8,128)S(1)} %get-tuple-element.99), channel_id=1, source_target_pairs={{0,2},{1,3},{2,0},{3,1},{4,6},{5,7},{6,4},{7,5}} | collective-permute-start | bytes 8847368 | tf_op jit(solution)/shard_map/ppermute | solution.py:141
  1319.0 154.8 %collective-permute-start.1 = (f32[144,5120]{1,0:T(8,128)}, f32[144,5120]{1,0:T(8,128)S(1)}, u32[]{:S(2)}, u32[]{:S(2)}) collective-permute-start(f32[144,5120]{1,0:T(8,128)} %get-tuple-element.96), channel_id=1, source_target_pairs={{0,2},{1,3},{2,0},{3,1},{4,6},{5,7},{6,4},{7,5}} | collective-permute-start | bytes 8847368 | tf_op jit(solution)/shard_map/ppermute | solution.py:141
  1319.6 154.7 %collective-permute-start.6 = (f32[144,5120]{1,0:T(8,128)}, f32[144,5120]{1,0:T(8,128)}, u32[]{:S(2)}, u32[]{:S(2)}) collective-permute-start(f32[144,5120]{1,0:T(8,128)} %get-tuple-element.97), channel_id=1, source_target_pairs={{0,4},{1,5},{2,6},{3,7},{4,0},{5,1},{6,2},{7,3}} | collective-permute-start | bytes 8847368 | tf_op jit(solution)/shard_map/ppermute | solution.py:141
  1417.5 120.0 %collective-permute-start.3 = (f32[144,5120]{1,0:T(8,128)}, f32[144,5120]{1,0:T(8,128)}, u32[]{:S(2)}, u32[]{:S(2)}) collective-permute-start(f32[144,5120]{1,0:T(8,128)} %get-tuple-element.100), channel_id=1, source_target_pairs={{0,4},{1,5},{2,6},{3,7},{4,0},{5,1},{6,2},{7,3}} | collective-permute-start | bytes 8847368 | tf_op jit(solution)/shard_map/ppermute | solution.py:141
  1418.5 119.0 %collective-permute-start.5 = (f32[144,5120]{1,0:T(8,128)}, f32[144,5120]{1,0:T(8,128)}, u32[]{:S(2)}, u32[]{:S(2)}) collective-permute-start(f32[144,5120]{1,0:T(8,128)} %get-tuple-element.101), channel_id=1, source_target_pairs={{0,2},{1,3},{2,0},{3,1},{4,6},{5,7},{6,4},{7,5}} | collective-permute-start | bytes 8847368 | tf_op jit(solution)/shard_map/ppermute | solution.py:141
  1429.4 217.2 %collective-permute-start.11 = (f32[144,5120]{1,0:T(8,128)}, f32[144,5120]{1,0:T(8,128)}, u32[]{:S(2)}, u32[]{:S(2)}) collective-permute-start(f32[144,5120]{1,0:T(8,128)} %get-tuple-element.92), channel_id=1, source_target_pairs={{0,4},{1,5},{2,6},{3,7},{4,0},{5,1},{6,2},{7,3}} | collective-permute-start | bytes 8847368 | tf_op jit(solution)/shard_map/ppermute | solution.py:141
  1473.8 172.8 %collective-permute-start.9 = (f32[144,5120]{1,0:T(8,128)}, f32[144,5120]{1,0:T(8,128)}, u32[]{:S(2)}, u32[]{:S(2)}) collective-permute-start(f32[144,5120]{1,0:T(8,128)} %get-tuple-element.93), channel_id=1, source_target_pairs={{0,2},{1,3},{2,0},{3,1},{4,6},{5,7},{6,4},{7,5}} | collective-permute-start | bytes 8847368 | tf_op jit(solution)/shard_map/ppermute | solution.py:141
  1545.6 976.9 %all-gather.22.cloned.1.call-start = ((), (), s32[]{:S(2)}) async-start(), calls=%async_computation.10 | async-start | bytes 26542080 | tf_op jit(solution)/shard_map/all_gather | solution.py:203
  1645.3 117.7 %collective-permute-start.8 = (f32[144,5120]{1,0:T(8,128)}, f32[144,5120]{1,0:T(8,128)}, u32[]{:S(2)}, u32[]{:S(2)}) collective-permute-start(f32[144,5120]{1,0:T(8,128)} %get-tuple-element.90), channel_id=1, source_target_pairs={{0,2},{1,3},{2,0},{3,1},{4,6},{5,7},{6,4},{7,5}} | collective-permute-start | bytes 8847368 | tf_op jit(solution)/shard_map/ppermute | solution.py:141
  1646.6 116.5 %collective-permute-start.13 = (f32[144,5120]{1,0:T(8,128)}, f32[144,5120]{1,0:T(8,128)}, u32[]{:S(2)}, u32[]{:S(2)}) collective-permute-start(f32[144,5120]{1,0:T(8,128)} %get-tuple-element.91), channel_id=1, source_target_pairs={{0,4},{1,5},{2,6},{3,7},{4,0},{5,1},{6,2},{7,3}} | collective-permute-start | bytes 8847368 | tf_op jit(solution)/shard_map/ppermute | solution.py:141
  1655.3 166.5 %collective-permute-start.10 = (f32[144,5120]{1,0:T(8,128)}, f32[144,5120]{1,0:T(8,128)}, u32[]{:S(2)}, u32[]{:S(2)}) collective-permute-start(f32[144,5120]{1,0:T(8,128)} %get-tuple-element.94), channel_id=1, source_target_pairs={{0,4},{1,5},{2,6},{3,7},{4,0},{5,1},{6,2},{7,3}} | collective-permute-start | bytes 8847368 | tf_op jit(solution)/shard_map/ppermute | solution.py:141
  1657.3 164.5 %collective-permute-start.12 = (f32[144,5120]{1,0:T(8,128)}, f32[144,5120]{1,0:T(8,128)}, u32[]{:S(2)}, u32[]{:S(2)}) collective-permute-start(f32[144,5120]{1,0:T(8,128)} %get-tuple-element.95), channel_id=1, source_target_pairs={{0,2},{1,3},{2,0},{3,1},{4,6},{5,7},{6,4},{7,5}} | collective-permute-start | bytes 8847368 | tf_op jit(solution)/shard_map/ppermute | solution.py:141
  1831.0 862.3 %all-gather.26.cloned.1.call-start = ((), (), s32[]{:S(2)}) async-start(), calls=%async_computation.12 | async-start | bytes 26542080 | tf_op jit(solution)/shard_map/all_gather | solution.py:203
  1933.3 19.9 collective-permute-start.14
  1962.0 66.8 %collective-permute-start.18 = (f32[144,5120]{1,0:T(8,128)S(1)}, f32[144,5120]{1,0:T(8,128)S(1)}, u32[]{:S(2)}, u32[]{:S(2)}) collective-permute-start(f32[144,5120]{1,0:T(8,128)S(1)} %get-tuple-element.86), channel_id=1, source_target_pairs={{0,4},{1,5},{2,6},{3,7},{4,0},{5,1},{6,2},{7,3}} | collective-permute-start | bytes 8847368 | tf_op jit(solution)/shard_map/ppermute | solution.py:141
  1962.4 66.8 %collective-permute-start.16 = (f32[144,5120]{1,0:T(8,128)S(1)}, f32[144,5120]{1,0:T(8,128)S(1)}, u32[]{:S(2)}, u32[]{:S(2)}) collective-permute-start(f32[144,5120]{1,0:T(8,128)S(1)} %get-tuple-element.87), channel_id=1, source_target_pairs={{0,2},{1,3},{2,0},{3,1},{4,6},{5,7},{6,4},{7,5}} | collective-permute-start | bytes 8847368 | tf_op jit(solution)/shard_map/ppermute | solution.py:141
  1963.7 142.4 %collective-permute-start.15 = (f32[144,5120]{1,0:T(8,128)}, f32[144,5120]{1,0:T(8,128)}, u32[]{:S(2)}, u32[]{:S(2)}) collective-permute-start(f32[144,5120]{1,0:T(8,128)} %get-tuple-element.84), channel_id=1, source_target_pairs={{0,2},{1,3},{2,0},{3,1},{4,6},{5,7},{6,4},{7,5}} | collective-permute-start | bytes 8847368 | tf_op jit(solution)/shard_map/ppermute | solution.py:141
  1964.4 141.7 %collective-permute-start.20 = (f32[144,5120]{1,0:T(8,128)}, f32[144,5120]{1,0:T(8,128)}, u32[]{:S(2)}, u32[]{:S(2)}) collective-permute-start(f32[144,5120]{1,0:T(8,128)} %get-tuple-element.85), channel_id=1, source_target_pairs={{0,4},{1,5},{2,6},{3,7},{4,0},{5,1},{6,2},{7,3}} | collective-permute-start | bytes 8847368 | tf_op jit(solution)/shard_map/ppermute | solution.py:141
  2035.8 118.9 %collective-permute-start.17 = (f32[144,5120]{1,0:T(8,128)}, f32[144,5120]{1,0:T(8,128)}, u32[]{:S(2)}, u32[]{:S(2)}) collective-permute-start(f32[144,5120]{1,0:T(8,128)} %get-tuple-element.88), channel_id=1, source_target_pairs={{0,4},{1,5},{2,6},{3,7},{4,0},{5,1},{6,2},{7,3}} | collective-permute-start | bytes 8847368 | tf_op jit(solution)/shard_map/ppermute | solution.py:141
  2037.4 117.3 %collective-permute-start.19 = (f32[144,5120]{1,0:T(8,128)}, f32[144,5120]{1,0:T(8,128)}, u32[]{:S(2)}, u32[]{:S(2)}) collective-permute-start(f32[144,5120]{1,0:T(8,128)} %get-tuple-element.89), channel_id=1, source_target_pairs={{0,2},{1,3},{2,0},{3,1},{4,6},{5,7},{6,4},{7,5}} | collective-permute-start | bytes 8847368 | tf_op jit(solution)/shard_map/ppermute | solution.py:141
  2163.6 550.0 %all-gather.30.cloned.1.call-start = ((), (), s32[]{:S(2)}) async-start(), calls=%async_computation.14 | async-start | bytes 17694720 | tf_op jit(solution)/shard_map/all_gather | solution.py:203
  2302.8 12.4 collective-permute-start.21
  2318.6 45.7 %collective-permute-start.25 = (f32[96,5120]{1,0:T(8,128)S(1)}, f32[96,5120]{1,0:T(8,128)S(1)}, u32[]{:S(2)}, u32[]{:S(2)}) collective-permute-start(f32[96,5120]{1,0:T(8,128)S(1)} %get-tuple-element.106), channel_id=1, source_target_pairs={{0,4},{1,5},{2,6},{3,7},{4,0},{5,1},{6,2},{7,3}} | collective-permute-start | bytes 5898248 | tf_op jit(solution)/shard_map/ppermute | solution.py:141
  2320.4 45.7 %collective-permute-start.23 = (f32[96,5120]{1,0:T(8,128)S(1)}, f32[96,5120]{1,0:T(8,128)S(1)}, u32[]{:S(2)}, u32[]{:S(2)}) collective-permute-start(f32[96,5120]{1,0:T(8,128)S(1)} %get-tuple-element.107), channel_id=1, source_target_pairs={{0,2},{1,3},{2,0},{3,1},{4,6},{5,7},{6,4},{7,5}} | collective-permute-start | bytes 5898248 | tf_op jit(solution)/shard_map/ppermute | solution.py:141
  2321.3 86.9 %collective-permute-start.22 = (f32[96,5120]{1,0:T(8,128)S(1)}, f32[96,5120]{1,0:T(8,128)S(1)}, u32[]{:S(2)}, u32[]{:S(2)}) collective-permute-start(f32[96,5120]{1,0:T(8,128)S(1)} %get-tuple-element.104), channel_id=1, source_target_pairs={{0,2},{1,3},{2,0},{3,1},{4,6},{5,7},{6,4},{7,5}} | collective-permute-start | bytes 5898248 | tf_op jit(solution)/shard_map/ppermute | solution.py:141
  2322.4 85.8 %collective-permute-start.27 = (f32[96,5120]{1,0:T(8,128)S(1)}, f32[96,5120]{1,0:T(8,128)S(1)}, u32[]{:S(2)}, u32[]{:S(2)}) collective-permute-start(f32[96,5120]{1,0:T(8,128)S(1)} %get-tuple-element.105), channel_id=1, source_target_pairs={{0,4},{1,5},{2,6},{3,7},{4,0},{5,1},{6,2},{7,3}} | collective-permute-start | bytes 5898248 | tf_op jit(solution)/shard_map/ppermute | solution.py:141
  2368.4 79.4 %collective-permute-start.24 = (f32[96,5120]{1,0:T(8,128)S(1)}, f32[96,5120]{1,0:T(8,128)S(1)}, u32[]{:S(2)}, u32[]{:S(2)}) collective-permute-start(f32[96,5120]{1,0:T(8,128)S(1)} %get-tuple-element.108), channel_id=1, source_target_pairs={{0,4},{1,5},{2,6},{3,7},{4,0},{5,1},{6,2},{7,3}} | collective-permute-start | bytes 5898248 | tf_op jit(solution)/shard_map/ppermute | solution.py:141
  2368.7 80.5 %collective-permute-start.26 = (f32[96,5120]{1,0:T(8,128)S(1)}, f32[96,5120]{1,0:T(8,128)S(1)}, u32[]{:S(2)}, u32[]{:S(2)}) collective-permute-start(f32[96,5120]{1,0:T(8,128)S(1)} %get-tuple-element.109), channel_id=1, source_target_pairs={{0,2},{1,3},{2,0},{3,1},{4,6},{5,7},{6,4},{7,5}} | collective-permute-start | bytes 5898248 | tf_op jit(solution)/shard_map/ppermute | solution.py:141
  2453.6 281.9 %all-gather.32.cloned.1.call-start = ((), (), s32[]{:S(2)}) async-start(), calls=%async_computation.15 | async-start | bytes 8847360 | tf_op jit(solution)/shard_map/all_gather | solution.py:203
  2619.7 24.6 collective-permute-start.32
  2621.1 24.6 collective-permute-start.30
  2622.1 44.7 %collective-permute-start.29 = (f32[48,5120]{1,0:T(8,128)S(1)}, f32[48,5120]{1,0:T(8,128)S(1)}, u32[]{:S(2)}, u32[]{:S(2)}) collective-permute-start(f32[48,5120]{1,0:T(8,128)S(1)} %get-tuple-element.112), channel_id=1, source_target_pairs={{0,2},{1,3},{2,0},{3,1},{4,6},{5,7},{6,4},{7,5}} | collective-permute-start | bytes 2949128 | tf_op jit(solution)/shard_map/ppermute | solution.py:141
  2623.1 43.7 %collective-permute-start.34 = (f32[48,5120]{1,0:T(8,128)S(1)}, f32[48,5120]{1,0:T(8,128)S(1)}, u32[]{:S(2)}, u32[]{:S(2)}) collective-permute-start(f32[48,5120]{1,0:T(8,128)S(1)} %get-tuple-element.113), channel_id=1, source_target_pairs={{0,4},{1,5},{2,6},{3,7},{4,0},{5,1},{6,2},{7,3}} | collective-permute-start | bytes 2949128 | tf_op jit(solution)/shard_map/ppermute | solution.py:141
  2646.0 39.6 %collective-permute-start.31 = (f32[48,5120]{1,0:T(8,128)S(1)}, f32[48,5120]{1,0:T(8,128)S(1)}, u32[]{:S(2)}, u32[]{:S(2)}) collective-permute-start(f32[48,5120]{1,0:T(8,128)S(1)} %get-tuple-element.116), channel_id=1, source_target_pairs={{0,4},{1,5},{2,6},{3,7},{4,0},{5,1},{6,2},{7,3}} | collective-permute-start | bytes 2949128 | tf_op jit(solution)/shard_map/ppermute | solution.py:141
  2646.7 40.0 %collective-permute-start.33 = (f32[48,5120]{1,0:T(8,128)S(1)}, f32[48,5120]{1,0:T(8,128)S(1)}, u32[]{:S(2)}, u32[]{:S(2)}) collective-permute-start(f32[48,5120]{1,0:T(8,128)S(1)} %get-tuple-element.117), channel_id=1, source_target_pairs={{0,2},{1,3},{2,0},{3,1},{4,6},{5,7},{6,4},{7,5}} | collective-permute-start | bytes 2949128 | tf_op jit(solution)/shard_map/ppermute | solution.py:141
  (33 other events, 696.1 us)
Sparse Core Ops, SparseCore 0:
  14.7 269.7 all-gather.11
  398.9 171.7 all-gather.15
  572.5 141.5 all-gather.19
  715.8 112.9 all-gather.23
  830.5 79.7 all-gather.27
  1306.6 76.4 all-gather.13
  1545.7 198.7 all-gather.17
  1831.1 114.4 all-gather.21
  2163.7 113.7 all-gather.25
  2453.7 79.1 all-gather.29
  2688.5 46.9 all-gather.31

commit v2 on v1

--- a/solution.py
+++ b/solution.py
@@ -10,23 +10,24 @@
 
 EPS = 1e-5
 ROPE_BASE = 10000.0
-CHUNKS = (6, 6, 6, 4, 2)
-SETTLED = 2
+CHUNKS = (6, 6, 5, 4, 3)
+PLACE_ROWS = 128
 Q_BLOCK = 128
 COL_TILE = 512
 
 
-def norm_rows(src_ref, dst_ref, gain_ref, rows, step):
-    gain = gain_ref[...].astype(jnp.float32)
-
+def norm_rows(src_ref, dst_ref, gain_ref, rows):
     def body(index, carry):
-        part = pl.ds(pl.multiple_of(index * step, step), step)
-        rows32 = src_ref[part, :].astype(jnp.float32)
-        inv_rms = lax.rsqrt(jnp.mean(rows32 * rows32, axis=-1, keepdims=True) + EPS)
-        dst_ref[part, :] = (rows32 * inv_rms * gain).astype(jnp.bfloat16)
+        parts = [pl.ds(pl.multiple_of(index * 48 + shift, 16), 16) for shift in (0, 16, 32)]
+        inv_rms = []
+        for part in parts:
+            rows32 = src_ref[part, :].astype(jnp.float32)
+            inv_rms.append(lax.rsqrt(jnp.mean(rows32 * rows32, axis=-1, keepdims=True) + EPS))
+        for part, inv in zip(parts, inv_rms):
+            dst_ref[part, :] = (src_ref[part, :].astype(jnp.float32) * inv * gain_ref[...].astype(jnp.float32)).astype(jnp.bfloat16)
         return carry
 
-    lax.fori_loop(0, rows // step, body, 0)
+    lax.fori_loop(0, rows // 48, body, 0)
 
 
 def attend_kernel(first, lens_ref, x_ref, wq_ref, wkv_ref, gain_ref, cos_ref, sin_ref, o_ref, k_ref, v_ref, normed_ref):
@@ -34,7 +35,7 @@
     head_dim = cos_ref.shape[1]
     group_size = wq_ref.shape[1] // head_dim
     length = lens_ref[first + pl.program_id(0)]
-    norm_rows(x_ref, normed_ref, gain_ref, seq_len, 16)
+    norm_rows(x_ref, normed_ref, gain_ref, seq_len)
     normed = normed_ref[...]
     kv_pre = jnp.dot(normed, wkv_ref[...], preferred_element_type=jnp.float32)
     q_pre = jnp.dot(normed, wq_ref[...], preferred_element_type=jnp.float32)
@@ -63,7 +64,7 @@
             scores = lax.dot_general(queries[j][lo:hi], keys[:hi], (((1,), (1,)), ((), ())), preferred_element_type=jnp.float32) * head_dim ** -0.5
             scores = jnp.where(allowed, scores, -jnp.inf)
             expd = jnp.exp(scores - jnp.max(scores, axis=-1, keepdims=True))
-            probs = (expd / jnp.sum(expd, axis=-1, keepdims=True)).astype(jnp.bfloat16)
+            probs = (expd * (1.0 / jnp.sum(expd, axis=-1, keepdims=True))).astype(jnp.bfloat16)
             o_ref[lo:hi, j * head_dim:(j + 1) * head_dim] = jnp.dot(probs, values[:hi], preferred_element_type=jnp.float32).astype(jnp.bfloat16)
 
 
@@ -109,7 +110,7 @@
 
     @pl.when(pl.program_id(0) == pl.num_programs(0) - 1)
     def _():
-        norm_rows(h_ref, n_ref, gain_ref, rows, 16)
+        norm_rows(h_ref, n_ref, gain_ref, rows)
 
 
 def project(o_all, w_out_all, x_rows, gain):
@@ -133,6 +134,26 @@
     )(o_all, w_out_all, x_rows, gain)
 
 
+def place_kernel(block_ref, *refs):
+    refs[-1][...] = block_ref[...]
+
+
+def place(y, block, start, total_rows):
+    rows, width = block.shape
+    operands = [block] if y is None else [block, y]
+    return pl.pallas_call(
+        place_kernel,
+        grid=(rows // PLACE_ROWS,),
+        in_specs=[pl.BlockSpec((PLACE_ROWS, width), lambda i: (i, 0)), pl.BlockSpec(memory_space=pl.ANY)][:len(operands)],
+        out_specs=pl.BlockSpec((PLACE_ROWS, width), lambda i: (start // PLACE_ROWS + i, 0)),
+        out_shape=jax.ShapeDtypeStruct((total_rows, width), jnp.bfloat16),
+        input_output_aliases={} if y is None else {1: 0},
+        compiler_params=pltpu.CompilerParams(vmem_limit_bytes=16 * 1024 * 1024),
+        cost_estimate=pl.CostEstimate(flops=rows * width, bytes_accessed=4 * rows * width, transcendentals=0),
+        name="place",
+    )(*operands)
+
+
 def solution(mesh):
     tp_size = mesh.shape["tp"]
     last = len(CHUNKS) - 1
@@ -145,14 +166,12 @@
         half = rows // 2
         me = lax.axis_index("tp")
         core, chip = me % 2, me // 2
-        blocks = partial.reshape(tp_size // 2, 2, rows, width)
-        take = lambda which: lax.dynamic_index_in_dim(blocks, which, 1, keepdims=False)
-        ours = take(core)
-        theirs = swap(take(1 - core), 1)
+        theirs = swap(partial, 1)
 
         def both(step, lo):
-            pick = lambda value: lax.dynamic_slice(value, (chip ^ step, lo, 0), (1, half, width))[0].astype(jnp.float32)
-            return pick(ours) + pick(theirs)
+            start = (2 * (chip ^ step) + core) * rows + lo
+            pick = lambda value: lax.dynamic_slice(value, (start, 0), (half, width)).astype(jnp.float32)
+            return pick(partial) + pick(theirs)
 
         x_far, y_far = swap(both(3, 0), 2), swap(both(3, half), 4)
         x_near, y_near = swap(both(1, 0), 2), swap(both(2, half), 4)
@@ -174,8 +193,12 @@
         cos_tab = jnp.cos(angles)
         sin_tab = jnp.sin(angles) * sign
         x_flat = x.reshape(batch_size * seq_len, width)
-        y = jnp.zeros((batch_size * seq_len, width), jnp.bfloat16)
+        y = None
         gathered = []
+
+        def settle(y, block, index):
+            return place(y, block, sum(CHUNKS[:index]) * seq_len, batch_size * seq_len)
+
         starts = [sum(CHUNKS[:index]) for index in range(len(CHUNKS))]
         attended, received = [], []
         for first, count in zip(starts, CHUNKS):
@@ -193,16 +216,14 @@
             gate_pre = jnp.dot(normed_all, w_gate, preferred_element_type=jnp.float32)
             up_pre = jnp.dot(normed_all, w_up, preferred_element_type=jnp.float32)
             gated = (jax.nn.silu(gate_pre) * up_pre).astype(jnp.bfloat16)
-            if index == last:
-                gated, settled = lax.optimization_barrier((gated, gathered[:SETTLED]))
-                for row, block in zip(starts, settled):
-                    y = lax.dynamic_update_slice(y, block, (row * seq_len, 0))
-                gated, y = lax.optimization_barrier((gated, y))
             mlp_part = jnp.dot(gated, w_down, preferred_element_type=jnp.float32).astype(jnp.bfloat16)
+            if index >= 2:
+                mlp_part, settled = lax.optimization_barrier((mlp_part, gathered[index - 2]))
+                y = settle(y, settled, index - 2)
             out_rows = sum_partials(mlp_part, hidden)
             gathered.append(lax.all_gather(out_rows, "tp", axis=0, tiled=True))
-        for index in range(SETTLED, len(CHUNKS)):
-            y = lax.dynamic_update_slice(y, gathered[index], (starts[index] * seq_len, 0))
+        for index in (last - 1, last):
+            y = settle(y, gathered[index], index)
         k_cache_out = lax.dynamic_update_slice(k_cache, jnp.concatenate(new_keys)[:, :, None, :], (0, 0, 0, 0))
         v_cache_out = lax.dynamic_update_slice(v_cache, jnp.concatenate(new_values)[:, :, None, :], (0, 0, 0, 0))
         return y.reshape(x.shape), k_cache_out, v_cache_out

time: 2760 us -> 2670 us (0.967)
  local copies, waits for them, and re-layouts: 173 us -> 73.7 us
  blocking collectives: 133 us -> 66 us
  waiting for transfers between devices: 627 us -> 668 us
    dynamic_update_slice x5 -> x0, local copies, waits for them, and re-layouts: 97.5 us -> none  [the longest x2 57.1 us: layer_shard(): y = lax.dynamic_update_slice(y, block, (row * seq_len, 0))]
    all_to_all x2 -> x1, blocking collectives: 133 us -> 66 us  [layer_shard(): lax.all_to_all(attended[-1][0].reshape(tp_size, count * seq_len // tp_siz...]
    all_to_all x3 -> x4, waiting for transfers between devices: 27.9 us -> 85.1 us  [layer_shard(): lax.all_to_all(attended[-1][0].reshape(tp_size, count * seq_len // tp_siz...]
    ppermute x35, waiting for transfers between devices: 590 us -> 543 us  [swap(): lax.ppermute(value, 'tp', [(index, index ^ bit) for index in range(tp_siz...]
    pallas_call x0 -> x5, Pallas kernels: none -> 44.2 us  [place(): pl.pallas_call(place_kernel, grid=(rows // PLACE_ROWS,), in_specs=[pl.Blo...]
    all_gather x5, waiting for transfers between devices: 0.06 us -> 40.1 us  [layer_shard(): normed_all = lax.all_gather(normed, 'tp', axis=0, tiled=True)]
    pallas_call x5, Pallas kernels: 329 us -> 291 us  [attend(): pl.pallas_call(functools.partial(attend_kernel, first), grid_spec=grid_sp...]
    squeeze x5 -> x0, local copies, waits for them, and re-layouts: 30.2 us -> none  [sum_partials(): lax.dynamic_index_in_dim(blocks, which, 1, keepdims=False)]
  transfers between devices with their start and end apart: 49 -> 50, of which waited for: 23 -> 22; matrix products, arithmetic and copies ran while one was open for 52% -> 51% of each run, Pallas kernels for 16% -> 16%
where the time goes in v2:
time: 2670 us; the launch traced here: 2660 us
  matrix products  1220 us (46%)
  waiting for transfers between devices  668 us (25%)
  Pallas kernels  467 us (17%)
  other arithmetic  108 us (4%)
  local copies, waits for them, and re-layouts  73.7 us (3%)
  blocking collectives  66 us (2%)
  starting transfers between devices  44.5 us (2%)
    ppermute x35, waiting for transfers between devices, swap(): lax.ppermute(value, 'tp', [(index, index ^ bit) for index in range(tp_siz...  543 us
    dot_general x5, matrix products, layer_shard(): up_pre = jnp.dot(normed_all, w_up, preferred_element_type=jnp.float32)  429 us
    dot_general x5, matrix products, layer_shard(): gate_pre = jnp.dot(normed_all, w_gate, preferred_element_type=jnp.float32)  402 us
    dot_general x5, matrix products, layer_shard(): jnp.dot(gated, w_down, preferred_element_type=jnp.float32)  390 us
    pallas_call x5, Pallas kernels, attend(): pl.pallas_call(functools.partial(attend_kernel, first), grid_spec=grid_sp...  291 us
    pallas_call x5, Pallas kernels, project(): pl.pallas_call(project_kernel, grid=(width // COL_TILE,), in_specs=[pl.Bl...  131 us
    all_to_all x4, waiting for transfers between devices, layer_shard(): lax.all_to_all(attended[-1][0].reshape(tp_size, count * seq_len // tp_siz...  85.1 us
    all_to_all x1, blocking collectives, layer_shard(): lax.all_to_all(attended[-1][0].reshape(tp_size, count * seq_len // tp_siz...  66 us
  transfers between devices with their start and end apart: 50, of which 22 were waited for; matrix products, arithmetic and copies ran while one was open for 51% of the time, Pallas kernels for 16%

profile of v2, /device:TPU:0, one launch (start us, length us, event | category | flops | bytes accessed | tf_op | source)
XLA Modules:
  0.0 2661.9 jit_solution(7188089719517969313)
XLA Ops:
  20.4 73.9 %attend.6 = (bf16[6,384,640]{2,1,0:T(8,128)(2,1)}, bf16[6,384,128]{2,1,0:T(8,128)(2,1)}, bf16[6,384,128]{2,1,0:T(8,128)(2,1)}) custom-call(s32[24]{0:T(128)} %lens_ref.9, bf16[24,384,5120]{2,1,0:T(8,128)(2,1)} %x_ref.9, bf16[5120,640]{1,0:T(8,128)(2,1)} %wq_ref.9, bf16[5120,256]{1,0:T(8,128)(2,1)} %copy-done.17, bf16[1,5120]{1,0:T(2,128)(2,1)} %broadcast_in_dim.52.gain_ref, ...), custom_call_target="tpu_custom_call" | custom-call | flops 21139292160 | bytes 26542080 | tf_op jit(solution)/shard_map/attend/pallas_call | solution.py:91
  98.5 38.3 %attend.5 = (bf16[3,384,640]{2,1,0:T(8,128)(2,1)}, bf16[3,384,128]{2,1,0:T(8,128)(2,1)}, bf16[3,384,128]{2,1,0:T(8,128)(2,1)}) custom-call(s32[24]{0:T(128)} %lens_ref.9, bf16[24,384,5120]{2,1,0:T(8,128)(2,1)} %x_ref.9, bf16[5120,640]{1,0:T(8,128)(2,1)} %wq_ref.9, bf16[5120,256]{1,0:T(8,128)(2,1)} %copy-done.17, bf16[1,5120]{1,0:T(2,128)(2,1)} %broadcast_in_dim.52.gain_ref, ...), custom_call_target="tpu_custom_call" | custom-call | flops 10569646080 | bytes 13271040 | tf_op jit(solution)/shard_map/attend/pallas_call | solution.py:91
  136.8 48.9 %attend.9 = (bf16[4,384,640]{2,1,0:T(8,128)(2,1)}, bf16[4,384,128]{2,1,0:T(8,128)(2,1)}, bf16[4,384,128]{2,1,0:T(8,128)(2,1)}) custom-call(s32[24]{0:T(128)} %lens_ref.9, bf16[24,384,5120]{2,1,0:T(8,128)(2,1)} %x_ref.9, bf16[5120,640]{1,0:T(8,128)(2,1)} %wq_ref.9, bf16[5120,256]{1,0:T(8,128)(2,1)} %copy-done.17, bf16[1,5120]{1,0:T(2,128)(2,1)} %broadcast_in_dim.52.gain_ref, ...), custom_call_target="tpu_custom_call" | custom-call | flops 14092861440 | bytes 17694720 | tf_op jit(solution)/shard_map/attend/pallas_call | solution.py:91
  185.7 60.0 %attend.8 = (bf16[5,384,640]{2,1,0:T(8,128)(2,1)}, bf16[5,384,128]{2,1,0:T(8,128)(2,1)}, bf16[5,384,128]{2,1,0:T(8,128)(2,1)}) custom-call(s32[24]{0:T(128)} %lens_ref.9, bf16[24,384,5120]{2,1,0:T(8,128)(2,1)} %x_ref.9, bf16[5120,640]{1,0:T(8,128)(2,1)} %wq_ref.9, bf16[5120,256]{1,0:T(8,128)(2,1)} %copy-done.17, bf16[1,5120]{1,0:T(2,128)(2,1)} %broadcast_in_dim.52.gain_ref, ...), custom_call_target="tpu_custom_call" | custom-call | flops 17616076800 | bytes 22118400 | tf_op jit(solution)/shard_map/attend/pallas_call | solution.py:91
  251.4 70.2 %attend.7 = (bf16[6,384,640]{2,1,0:T(8,128)(2,1)}, bf16[6,384,128]{2,1,0:T(8,128)(2,1)}, bf16[6,384,128]{2,1,0:T(8,128)(2,1)}) custom-call(s32[24]{0:T(128)} %lens_ref.9, bf16[24,384,5120]{2,1,0:T(8,128)(2,1)} %x_ref.9, bf16[5120,640]{1,0:T(8,128)(2,1)} %wq_ref.9, bf16[5120,256]{1,0:T(8,128)(2,1)} %copy-done.17, bf16[1,5120]{1,0:T(2,128)(2,1)} %broadcast_in_dim.52.gain_ref, ...), custom_call_target="tpu_custom_call" | custom-call | flops 21139292160 | bytes 26542080 | tf_op jit(solution)/shard_map/attend/pallas_call | solution.py:91
  323.1 28.4 %project.7 = (bf16[288,5120]{1,0:T(8,128)(2,1)S(1)}, bf16[288,5120]{1,0:T(8,128)(2,1)S(1)}) custom-call(bf16[8,288,640]{2,1,0:T(8,128)(2,1)} %copy-done.18, bf16[5120,5120]{1,0:T(8,128)(2,1)} %all-gather.12.cloned.1.call-done.w_ref, bf16[288,5120]{1,0:T(8,128)(2,1)} %get-tuple-element.78.x_ref, bf16[1,5120]{1,0:T(2,128)(2,1)S(1)} %broadcast_in_dim.57.gain_ref), custom_call_target="tpu_custom_call" | custom-call | flops 15099494400 | bytes 64225280 | tf_op jit(solution)/shard_map/project/pallas_call | solution.py:120
  353.2 66.0 %all_to_all.25.o_ref = bf16[8,288,640]{2,1,0:T(8,128)(2,1)} all-to-all(bf16[8,288,640]{2,1,0:T(8,128)(2,1)} %bitcast.52), channel_id=1, replica_groups=mesh['dp'=1,'tp'=8] {'tp'}, dimensions={0} | all-to-all | bytes 5898240 | tf_op jit(solution)/shard_map/all_to_all | solution.py:206
  419.2 31.0 %project.9 = (bf16[288,5120]{1,0:T(8,128)(2,1)S(1)}, bf16[288,5120]{1,0:T(8,128)(2,1)S(1)}) custom-call(bf16[8,288,640]{2,1,0:T(8,128)(2,1)} %all_to_all.25.o_ref, bf16[5120,5120]{1,0:T(8,128)(2,1)} %all-gather.12.cloned.1.call-done.w_ref, bf16[288,5120]{1,0:T(8,128)(2,1)} %get-tuple-element.77.x_ref, bf16[1,5120]{1,0:T(2,128)(2,1)S(1)} %broadcast_in_dim.57.gain_ref), custom_call_target="tpu_custom_call" | custom-call | flops 15099494400 | bytes 64225280 | tf_op jit(solution)/shard_map/project/pallas_call | solution.py:120
  453.6 40.1 %all-gather.18.cloned.1.call-done = bf16[2304,5120]{1,0:T(8,128)(2,1)} async-done(((bf16[288,5120]{1,0:T(8,128)(2,1)}), bf16[2304,5120]{1,0:T(8,128)(2,1)}) %all-gather.18.cloned.1.call-update) | async-done | bytes 23592976 | tf_op jit(solution)/shard_map/all_gather | solution.py:215
  493.7 101.3 %fusion.3 = f32[2304,3456]{1,0:T(8,128)} fusion(bf16[2304,5120]{1,0:T(8,128)(2,1)} %all-gather.18.cloned.1.call-done, bf16[5120,3456]{1,0:T(8,128)(2,1)} %param.19), kind=kOutput, calls=%fused_computation.84 | convolution fusion | flops 81537269760 | bytes 90832896 | tf_op jit(solution)/shard_map/dot_general | solution.py:216
  595.0 104.8 %multiply_convert_fusion.1 = bf16[2304,3456]{1,0:T(8,128)(2,1)} fusion(f32[2304,3456]{1,0:T(8,128)} %fusion.3, bf16[2304,5120]{1,0:T(8,128)(2,1)} %all-gather.18.cloned.1.call-done, bf16[5120,3456]{1,0:T(8,128)(2,1)} %param.20), kind=kOutput, calls=%fused_computation.1 | convolution fusion | flops 81585045504 | bytes 106758144 | tf_op jit(solution)/shard_map/dot_general | solution.py:217
  699.8 95.1 %convolution_convert_fusion.1 = bf16[2304,5120]{1,0:T(8,128)(2,1)} fusion(bf16[2304,3456]{1,0:T(8,128)(2,1)} %multiply_convert_fusion.1, bf16[3456,5120]{1,0:T(8,128)(2,1)} %param.21), kind=kOutput, calls=%fused_computation.3 | convolution fusion | flops 81549066240 | bytes 74907648 | tf_op jit(solution)/shard_map/dot_general | solution.py:219
  801.4 29.1 %all-to-all-done.1.o_ref = bf16[8,240,640]{2,1,0:T(8,128)(2,1)} async-done(((bf16[8,240,640]{2,1,0:T(8,128)(2,1)}), bf16[8,240,640]{2,1,0:T(8,128)(2,1)}, u32[]{:S(2)}, u32[]{:S(2)}) %all-to-all-start.1) | async-done | bytes 2457632 | tf_op jit(solution)/shard_map/all_to_all | solution.py:206
  830.5 26.0 project.6
  860.0 11.0 convert_add_fusion.7
  875.0 116.7 %collective-permute-done.2 = f32[144,5120]{1,0:T(8,128)} collective-permute-done((f32[144,5120]{1,0:T(8,128)}, f32[144,5120]{1,0:T(8,128)}, u32[]{:S(2)}, u32[]{:S(2)}) %collective-permute-start.2) | collective-permute-done | bytes 2949152 | tf_op jit(solution)/shard_map/ppermute | solution.py:162
  1002.9 96.6 %fusion.5 = f32[2304,3456]{1,0:T(8,128)} fusion(bf16[2304,5120]{1,0:T(8,128)(2,1)} %all-gather.28.cloned.1.call-done, bf16[5120,3456]{1,0:T(8,128)(2,1)} %param.19), kind=kOutput, calls=%fused_computation.86 | convolution fusion | flops 81537269760 | bytes 90832896 | tf_op jit(solution)/shard_map/dot_general | solution.py:216
  1099.5 38.0 %collective-permute-done.3 = f32[144,5120]{1,0:T(8,128)} collective-permute-done((f32[144,5120]{1,0:T(8,128)}, f32[144,5120]{1,0:T(8,128)}, u32[]{:S(2)}, u32[]{:S(2)}) %collective-permute-start.3) | collective-permute-done | bytes 2949152 | tf_op jit(solution)/shard_map/ppermute | solution.py:162
  1146.5 107.7 %multiply_convert_fusion = bf16[2304,3456]{1,0:T(8,128)(2,1)} fusion(f32[2304,3456]{1,0:T(8,128)} %fusion.5, bf16[2304,5120]{1,0:T(8,128)(2,1)} %all-gather.28.cloned.1.call-done, bf16[5120,3456]{1,0:T(8,128)(2,1)} %param.20), kind=kOutput, calls=%fused_computation | convolution fusion | flops 81585045504 | bytes 106758144 | tf_op jit(solution)/shard_map/dot_general | solution.py:217
  1254.2 95.0 %convolution_convert_fusion = bf16[2304,5120]{1,0:T(8,128)(2,1)} fusion(bf16[2304,3456]{1,0:T(8,128)(2,1)} %multiply_convert_fusion, bf16[3456,5120]{1,0:T(8,128)(2,1)} %param.21), kind=kOutput, calls=%fused_computation.2 | convolution fusion | flops 81549066240 | bytes 74907648 | tf_op jit(solution)/shard_map/dot_general | solution.py:219
  1354.6 30.1 %all-to-all-done.3.o_ref = bf16[8,192,640]{2,1,0:T(8,128)(2,1)S(1)} async-done(((bf16[8,192,640]{2,1,0:T(8,128)(2,1)}), bf16[8,192,640]{2,1,0:T(8,128)(2,1)S(1)}, u32[]{:S(2)}, u32[]{:S(2)}) %all-to-all-start.3) | async-done | bytes 1966112 | tf_op jit(solution)/shard_map/all_to_all | solution.py:206
  1384.7 23.6 project.8
  1411.0 9.2 convert_add_fusion.3
  1424.3 120.1 %collective-permute-done.23 = f32[144,5120]{1,0:T(8,128)S(1)} collective-permute-done((f32[144,5120]{1,0:T(8,128)S(1)}, f32[144,5120]{1,0:T(8,128)S(1)}, u32[]{:S(2)}, u32[]{:S(2)}) %collective-permute-start.23) | collective-permute-done | bytes 2949152 | tf_op jit(solution)/shard_map/ppermute | solution.py:162
  1554.2 83.2 %fusion.2 = f32[1920,3456]{1,0:T(8,128)} fusion(bf16[1920,5120]{1,0:T(8,128)(2,1)} %all-gather.16.cloned.1.call-done, bf16[5120,3456]{1,0:T(8,128)(2,1)} %param.19), kind=kOutput, calls=%fused_computation.83 | convolution fusion | flops 67947724800 | bytes 81592320 | tf_op jit(solution)/shard_map/dot_general | solution.py:216
  1637.4 36.1 %collective-permute-done.24 = f32[144,5120]{1,0:T(8,128)} collective-permute-done((f32[144,5120]{1,0:T(8,128)}, f32[144,5120]{1,0:T(8,128)}, u32[]{:S(2)}, u32[]{:S(2)}) %collective-permute-start.24) | collective-permute-done | bytes 2949152 | tf_op jit(solution)/shard_map/ppermute | solution.py:162
  1682.4 90.8 %multiply_convert_fusion.2 = bf16[1920,3456]{1,0:T(8,128)(2,1)} fusion(f32[1920,3456]{1,0:T(8,128)} %fusion.2, bf16[1920,5120]{1,0:T(8,128)(2,1)} %all-gather.16.cloned.1.call-done, bf16[5120,3456]{1,0:T(8,128)(2,1)} %param.20), kind=kOutput, calls=%fused_computation.4 | convolution fusion | flops 67987537920 | bytes 94863360 | tf_op jit(solution)/shard_map/dot_general | solution.py:217
  1773.2 82.0 %convolution_convert_fusion.2 = bf16[1920,5120]{1,0:T(8,128)(2,1)} fusion(bf16[1920,3456]{1,0:T(8,128)(2,1)} %multiply_convert_fusion.2, bf16[3456,5120]{1,0:T(8,128)(2,1)} %param.21), kind=kOutput, calls=%fused_computation.7 | convolution fusion | flops 67957555200 | bytes 68321280 | tf_op jit(solution)/shard_map/dot_general | solution.py:219
  1859.1 25.9 all-to-all-done.o_ref
  1884.9 22.1 project.5
  1909.5 68.5 %fusion.4 = f32[1536,3456]{1,0:T(8,128)} fusion(bf16[1536,5120]{1,0:T(8,128)(2,1)} %all-gather.26.cloned.1.call-done, bf16[5120,3456]{1,0:T(8,128)(2,1)} %param.19), kind=kOutput, calls=%fused_computation.85 | convolution fusion | flops 54358179840 | bytes 72351744 | tf_op jit(solution)/shard_map/dot_general | solution.py:216
  1987.2 71.4 %multiply_convert_fusion.3 = bf16[1536,3456]{1,0:T(8,128)(2,1)} fusion(f32[1536,3456]{1,0:T(8,128)} %fusion.4, bf16[1536,5120]{1,0:T(8,128)(2,1)} %all-gather.26.cloned.1.call-done, bf16[5120,3456]{1,0:T(8,128)(2,1)} %param.20), kind=kOutput, calls=%fused_computation.5 | convolution fusion | flops 54390030336 | bytes 82968576 | tf_op jit(solution)/shard_map/dot_general | solution.py:217
  2068.4 66.1 %convolution_convert_fusion.4 = bf16[1536,5120]{1,0:T(8,128)(2,1)} fusion(bf16[1536,3456]{1,0:T(8,128)(2,1)} %multiply_convert_fusion.3, bf16[3456,5120]{1,0:T(8,128)(2,1)} %param.21), kind=kOutput, calls=%fused_computation.9 | convolution fusion | flops 54366044160 | bytes 61734912 | tf_op jit(solution)/shard_map/dot_general | solution.py:219
  2134.5 32.8 %collective-permute-done.10 = f32[120,5120]{1,0:T(8,128)} collective-permute-done((f32[120,5120]{1,0:T(8,128)}, f32[120,5120]{1,0:T(8,128)}, u32[]{:S(2)}, u32[]{:S(2)}) %collective-permute-start.10) | collective-permute-done | bytes 2457632 | tf_op jit(solution)/shard_map/ppermute | solution.py:162
  2185.5 52.1 %fusion.1 = f32[1152,3456]{1,0:T(8,128)} fusion(bf16[1152,5120]{1,0:T(8,128)(2,1)} %all-gather.14.cloned.1.call-done, bf16[5120,3456]{1,0:T(8,128)(2,1)} %param.19), kind=kOutput, calls=%fused_computation.82 | convolution fusion | flops 40768634880 | bytes 63111168 | tf_op jit(solution)/shard_map/dot_general | solution.py:216
  2239.6 25.6 collective-permute-done.30
  2273.1 54.1 %fusion = bf16[1152,3456]{1,0:T(8,128)(2,1)} fusion(bf16[1152,5120]{1,0:T(8,128)(2,1)} %all-gather.14.cloned.1.call-done, bf16[5120,3456]{1,0:T(8,128)(2,1)} %param.20, f32[1152,3456]{1,0:T(8,128)} %fusion.1), kind=kOutput, calls=%fused_computation.10 | convolution fusion | flops 40792522752 | bytes 71073792 | tf_op jit(solution)/shard_map/dot_general | solution.py:217
  2327.1 22.3 collective-permute-done.29
  2350.2 40.0 %collective-permute-done.31 = f32[96,5120]{1,0:T(8,128)S(1)} collective-permute-done((f32[96,5120]{1,0:T(8,128)S(1)}, f32[96,5120]{1,0:T(8,128)S(1)}, u32[]{:S(2)}, u32[]{:S(2)}) %collective-permute-start.31) | collective-permute-done | bytes 1966112 | tf_op jit(solution)/shard_map/ppermute | solution.py:162
  2395.2 51.6 %convolution_convert_fusion.3 = bf16[1152,5120]{1,0:T(8,128)(2,1)} fusion(bf16[1152,3456]{1,0:T(8,128)(2,1)} %fusion, bf16[3456,5120]{1,0:T(8,128)(2,1)} %param.21), kind=kOutput, calls=%fused_computation.8 | convolution fusion | flops 40774533120 | bytes 55148544 | tf_op jit(solution)/shard_map/dot_general | solution.py:219
  2446.8 20.8 collective-permute-done.14
  2476.9 31.4 %collective-permute-done.16 = f32[72,5120]{1,0:T(8,128)} collective-permute-done((f32[72,5120]{1,0:T(8,128)}, f32[72,5120]{1,0:T(8,128)}, u32[]{:S(2)}, u32[]{:S(2)}) %collective-permute-start.16) | collective-permute-done | bytes 1474592 | tf_op jit(solution)/shard_map/ppermute | solution.py:162
  2516.3 23.6 collective-permute-done.15
  2540.3 30.6 %collective-permute-done.17 = f32[72,5120]{1,0:T(8,128)} collective-permute-done((f32[72,5120]{1,0:T(8,128)}, f32[72,5120]{1,0:T(8,128)}, u32[]{:S(2)}, u32[]{:S(2)}) %collective-permute-start.17) | collective-permute-done | bytes 1474592 | tf_op jit(solution)/shard_map/ppermute | solution.py:162
  2582.4 8.4 copy-done
  2590.9 11.5 place.5.refs_0_
  2605.9 10.7 place.6.refs_0_
  2623.2 9.1 place.7.refs_0_
  (229 shorter events, 215.3 us)
Async XLA Ops:
  7.2 314.4 %all-gather.12.cloned.1.call-start = ((), (), s32[]{:S(2)}) async-start(), calls=%async_computation.5 | async-start | bytes 58982400 | tf_op jit(solution)/shard_map/all_gather | solution.py:188
  94.3 227.3 %all-to-all-start.2 = ((bf16[8,288,640]{2,1,0:T(8,128)(2,1)}), bf16[8,288,640]{2,1,0:T(8,128)(2,1)S(1)}, u32[]{:S(2)}, u32[]{:S(2)}) async-start(bf16[8,288,640]{2,1,0:T(8,128)(2,1)} %bitcast.51), calls=%async_computation.2 | async-start | bytes 5898240 | tf_op jit(solution)/shard_map/all_to_all | solution.py:206
  98.3 395.4 %all-gather.18.cloned.1.call-start = ((), (), s32[]{:S(2)}) async-start(), calls=%async_computation.8 | async-start | bytes 26542080 | tf_op jit(solution)/shard_map/all_gather | solution.py:215
  353.1 649.8 %all-gather.28.cloned.1.call-start = ((), (), s32[]{:S(2)}) async-start(), calls=%async_computation.13 | async-start | bytes 26542080 | tf_op jit(solution)/shard_map/all_gather | solution.py:215
  794.9 65.1 %collective-permute-start = (bf16[2304,5120]{1,0:T(8,128)(2,1)}, bf16[2304,5120]{1,0:T(8,128)(2,1)}, u32[]{:S(2)}, u32[]{:S(2)}) collective-permute-start(bf16[2304,5120]{1,0:T(8,128)(2,1)} %convolution_convert_fusion.1), channel_id=1, source_target_pairs={{0,1},{1,0},{2,3},{3,2},{4,5},{5,4},{6,7},{7,6}} | collective-permute-start | bytes 70778888 | tf_op jit(solution)/shard_map/ppermute | solution.py:162
  794.9 35.6 %all-to-all-start.1 = ((bf16[8,240,640]{2,1,0:T(8,128)(2,1)}), bf16[8,240,640]{2,1,0:T(8,128)(2,1)}, u32[]{:S(2)}, u32[]{:S(2)}) async-start(bf16[8,240,640]{2,1,0:T(8,128)(2,1)} %bitcast.53), calls=%async_computation.1 | async-start | bytes 4915200 | tf_op jit(solution)/shard_map/all_to_all | solution.py:206
  798.1 756.1 %all-gather.16.cloned.1.call-start = ((), (), s32[]{:S(2)}) async-start(), calls=%async_computation.7 | async-start | bytes 22118400 | tf_op jit(solution)/shard_map/all_gather | solution.py:215
  859.4 995.7 %all-gather.20.cloned.1.call-start = ((), (), s32[]{:S(2)}) async-start(), calls=%async_computation.9 | async-start | bytes 26542080 | tf_op jit(solution)/shard_map/all_gather | solution.py:224
  870.9 120.7 %collective-permute-start.2 = (f32[144,5120]{1,0:T(8,128)}, f32[144,5120]{1,0:T(8,128)}, u32[]{:S(2)}, u32[]{:S(2)}) collective-permute-start(f32[144,5120]{1,0:T(8,128)} %get-tuple-element.92), channel_id=1, source_target_pairs={{0,2},{1,3},{2,0},{3,1},{4,6},{5,7},{6,4},{7,5}} | collective-permute-start | bytes 8847368 | tf_op jit(solution)/shard_map/ppermute | solution.py:162
  871.4 121.2 %collective-permute-start.4 = (f32[144,5120]{1,0:T(8,128)}, f32[144,5120]{1,0:T(8,128)}, u32[]{:S(2)}, u32[]{:S(2)}) collective-permute-start(f32[144,5120]{1,0:T(8,128)} %get-tuple-element.91), channel_id=1, source_target_pairs={{0,4},{1,5},{2,6},{3,7},{4,0},{5,1},{6,2},{7,3}} | collective-permute-start | bytes 8847368 | tf_op jit(solution)/shard_map/ppermute | solution.py:162
  871.4 228.2 %collective-permute-start.1 = (f32[144,5120]{1,0:T(8,128)}, f32[144,5120]{1,0:T(8,128)}, u32[]{:S(2)}, u32[]{:S(2)}) collective-permute-start(f32[144,5120]{1,0:T(8,128)} %get-tuple-element.89), channel_id=1, source_target_pairs={{0,2},{1,3},{2,0},{3,1},{4,6},{5,7},{6,4},{7,5}} | collective-permute-start | bytes 8847368 | tf_op jit(solution)/shard_map/ppermute | solution.py:162
  873.0 226.6 %collective-permute-start.6 = (f32[144,5120]{1,0:T(8,128)}, f32[144,5120]{1,0:T(8,128)}, u32[]{:S(2)}, u32[]{:S(2)}) collective-permute-start(f32[144,5120]{1,0:T(8,128)} %get-tuple-element.90), channel_id=1, source_target_pairs={{0,4},{1,5},{2,6},{3,7},{4,0},{5,1},{6,2},{7,3}} | collective-permute-start | bytes 8847368 | tf_op jit(solution)/shard_map/ppermute | solution.py:162
  1000.8 136.8 %collective-permute-start.3 = (f32[144,5120]{1,0:T(8,128)}, f32[144,5120]{1,0:T(8,128)}, u32[]{:S(2)}, u32[]{:S(2)}) collective-permute-start(f32[144,5120]{1,0:T(8,128)} %get-tuple-element.93), channel_id=1, source_target_pairs={{0,4},{1,5},{2,6},{3,7},{4,0},{5,1},{6,2},{7,3}} | collective-permute-start | bytes 8847368 | tf_op jit(solution)/shard_map/ppermute | solution.py:162
  1002.4 135.2 %collective-permute-start.5 = (f32[144,5120]{1,0:T(8,128)}, f32[144,5120]{1,0:T(8,128)}, u32[]{:S(2)}, u32[]{:S(2)}) collective-permute-start(f32[144,5120]{1,0:T(8,128)} %get-tuple-element.94), channel_id=1, source_target_pairs={{0,2},{1,3},{2,0},{3,1},{4,6},{5,7},{6,4},{7,5}} | collective-permute-start | bytes 8847368 | tf_op jit(solution)/shard_map/ppermute | solution.py:162
  1349.3 61.7 %collective-permute-start.21 = (bf16[2304,5120]{1,0:T(8,128)(2,1)}, bf16[2304,5120]{1,0:T(8,128)(2,1)}, u32[]{:S(2)}, u32[]{:S(2)}) collective-permute-start(bf16[2304,5120]{1,0:T(8,128)(2,1)} %convolution_convert_fusion), channel_id=1, source_target_pairs={{0,1},{1,0},{2,3},{3,2},{4,5},{5,4},{6,7},{7,6}} | collective-permute-start | bytes 70778888 | tf_op jit(solution)/shard_map/ppermute | solution.py:162
  1349.3 35.5 %all-to-all-start.3 = ((bf16[8,192,640]{2,1,0:T(8,128)(2,1)}), bf16[8,192,640]{2,1,0:T(8,128)(2,1)S(1)}, u32[]{:S(2)}, u32[]{:S(2)}) async-start(bf16[8,192,640]{2,1,0:T(8,128)(2,1)} %bitcast.54), calls=%async_computation.3 | async-start | bytes 3932160 | tf_op jit(solution)/shard_map/all_to_all | solution.py:206
  1351.6 557.9 %all-gather.26.cloned.1.call-start = ((), (), s32[]{:S(2)}) async-start(), calls=%async_computation.12 | async-start | bytes 17694720 | tf_op jit(solution)/shard_map/all_gather | solution.py:215
  1411.0 723.6 %all-gather.30.cloned.1.call-start = ((), (), s32[]{:S(2)}) async-start(), calls=%async_computation.14 | async-start | bytes 26542080 | tf_op jit(solution)/shard_map/all_gather | solution.py:224
  1420.2 124.1 %collective-permute-start.23 = (f32[144,5120]{1,0:T(8,128)S(1)}, f32[144,5120]{1,0:T(8,128)S(1)}, u32[]{:S(2)}, u32[]{:S(2)}) collective-permute-start(f32[144,5120]{1,0:T(8,128)S(1)} %get-tuple-element.86), channel_id=1, source_target_pairs={{0,2},{1,3},{2,0},{3,1},{4,6},{5,7},{6,4},{7,5}} | collective-permute-start | bytes 8847368 | tf_op jit(solution)/shard_map/ppermute | solution.py:162
  1421.9 123.6 %collective-permute-start.25 = (f32[144,5120]{1,0:T(8,128)S(1)}, f32[144,5120]{1,0:T(8,128)S(1)}, u32[]{:S(2)}, u32[]{:S(2)}) collective-permute-start(f32[144,5120]{1,0:T(8,128)S(1)} %get-tuple-element.85), channel_id=1, source_target_pairs={{0,4},{1,5},{2,6},{3,7},{4,0},{5,1},{6,2},{7,3}} | collective-permute-start | bytes 8847368 | tf_op jit(solution)/shard_map/ppermute | solution.py:162
  1422.1 215.3 %collective-permute-start.22 = (f32[144,5120]{1,0:T(8,128)}, f32[144,5120]{1,0:T(8,128)}, u32[]{:S(2)}, u32[]{:S(2)}) collective-permute-start(f32[144,5120]{1,0:T(8,128)} %get-tuple-element.83), channel_id=1, source_target_pairs={{0,2},{1,3},{2,0},{3,1},{4,6},{5,7},{6,4},{7,5}} | collective-permute-start | bytes 8847368 | tf_op jit(solution)/shard_map/ppermute | solution.py:162
  1423.1 214.3 %collective-permute-start.27 = (f32[144,5120]{1,0:T(8,128)}, f32[144,5120]{1,0:T(8,128)}, u32[]{:S(2)}, u32[]{:S(2)}) collective-permute-start(f32[144,5120]{1,0:T(8,128)} %get-tuple-element.84), channel_id=1, source_target_pairs={{0,4},{1,5},{2,6},{3,7},{4,0},{5,1},{6,2},{7,3}} | collective-permute-start | bytes 8847368 | tf_op jit(solution)/shard_map/ppermute | solution.py:162
  1552.1 121.4 %collective-permute-start.24 = (f32[144,5120]{1,0:T(8,128)}, f32[144,5120]{1,0:T(8,128)}, u32[]{:S(2)}, u32[]{:S(2)}) collective-permute-start(f32[144,5120]{1,0:T(8,128)} %get-tuple-element.87), channel_id=1, source_target_pairs={{0,4},{1,5},{2,6},{3,7},{4,0},{5,1},{6,2},{7,3}} | collective-permute-start | bytes 8847368 | tf_op jit(solution)/shard_map/ppermute | solution.py:162
  1552.4 121.1 %collective-permute-start.26 = (f32[144,5120]{1,0:T(8,128)}, f32[144,5120]{1,0:T(8,128)}, u32[]{:S(2)}, u32[]{:S(2)}) collective-permute-start(f32[144,5120]{1,0:T(8,128)} %get-tuple-element.88), channel_id=1, source_target_pairs={{0,2},{1,3},{2,0},{3,1},{4,6},{5,7},{6,4},{7,5}} | collective-permute-start | bytes 8847368 | tf_op jit(solution)/shard_map/ppermute | solution.py:162
  1855.2 122.8 %collective-permute-start.7 = (bf16[1920,5120]{1,0:T(8,128)(2,1)}, bf16[1920,5120]{1,0:T(8,128)(2,1)}, u32[]{:S(2)}, u32[]{:S(2)}) collective-permute-start(bf16[1920,5120]{1,0:T(8,128)(2,1)} %convolution_convert_fusion.2), channel_id=1, source_target_pairs={{0,1},{1,0},{2,3},{3,2},{4,5},{5,4},{6,7},{7,6}} | collective-permute-start | bytes 58982408 | tf_op jit(solution)/shard_map/ppermute | solution.py:162
  1857.5 328.0 %all-gather.14.cloned.1.call-start = ((), (), s32[]{:S(2)}) async-start(), calls=%async_computation.6 | async-start | bytes 13271040 | tf_op jit(solution)/shard_map/all_gather | solution.py:215
  1909.4 537.4 %all-gather.22.cloned.1.call-start = ((), (), s32[]{:S(2)}) async-start(), calls=%async_computation.10 | async-start | bytes 22118400 | tf_op jit(solution)/shard_map/all_gather | solution.py:224
  1986.0 75.4 %collective-permute-start.9 = (f32[120,5120]{1,0:T(8,128)S(1)}, f32[120,5120]{1,0:T(8,128)S(1)}, u32[]{:S(2)}, u32[]{:S(2)}) collective-permute-start(f32[120,5120]{1,0:T(8,128)S(1)} %get-tuple-element.100), channel_id=1, source_target_pairs={{0,2},{1,3},{2,0},{3,1},{4,6},{5,7},{6,4},{7,5}} | collective-permute-start | bytes 7372808 | tf_op jit(solution)/shard_map/ppermute | solution.py:162
  1987.2 74.2 %collective-permute-start.11 = (f32[120,5120]{1,0:T(8,128)S(1)}, f32[120,5120]{1,0:T(8,128)S(1)}, u32[]{:S(2)}, u32[]{:S(2)}) collective-permute-start(f32[120,5120]{1,0:T(8,128)S(1)} %get-tuple-element.99), channel_id=1, source_target_pairs={{0,4},{1,5},{2,6},{3,7},{4,0},{5,1},{6,2},{7,3}} | collective-permute-start | bytes 7372808 | tf_op jit(solution)/shard_map/ppermute | solution.py:162
  2058.6 75.9 %collective-permute-start.8 = (f32[120,5120]{1,0:T(8,128)}, f32[120,5120]{1,0:T(8,128)}, u32[]{:S(2)}, u32[]{:S(2)}) collective-permute-start(f32[120,5120]{1,0:T(8,128)} %get-tuple-element.97), channel_id=1, source_target_pairs={{0,2},{1,3},{2,0},{3,1},{4,6},{5,7},{6,4},{7,5}} | collective-permute-start | bytes 7372808 | tf_op jit(solution)/shard_map/ppermute | solution.py:162
  2059.8 74.7 %collective-permute-start.13 = (f32[120,5120]{1,0:T(8,128)}, f32[120,5120]{1,0:T(8,128)}, u32[]{:S(2)}, u32[]{:S(2)}) collective-permute-start(f32[120,5120]{1,0:T(8,128)} %get-tuple-element.98), channel_id=1, source_target_pairs={{0,4},{1,5},{2,6},{3,7},{4,0},{5,1},{6,2},{7,3}} | collective-permute-start | bytes 7372808 | tf_op jit(solution)/shard_map/ppermute | solution.py:162
  2067.1 100.2 %collective-permute-start.10 = (f32[120,5120]{1,0:T(8,128)}, f32[120,5120]{1,0:T(8,128)}, u32[]{:S(2)}, u32[]{:S(2)}) collective-permute-start(f32[120,5120]{1,0:T(8,128)} %get-tuple-element.101), channel_id=1, source_target_pairs={{0,4},{1,5},{2,6},{3,7},{4,0},{5,1},{6,2},{7,3}} | collective-permute-start | bytes 7372808 | tf_op jit(solution)/shard_map/ppermute | solution.py:162
  2067.6 99.8 %collective-permute-start.12 = (f32[120,5120]{1,0:T(8,128)}, f32[120,5120]{1,0:T(8,128)}, u32[]{:S(2)}, u32[]{:S(2)}) collective-permute-start(f32[120,5120]{1,0:T(8,128)} %get-tuple-element.102), channel_id=1, source_target_pairs={{0,2},{1,3},{2,0},{3,1},{4,6},{5,7},{6,4},{7,5}} | collective-permute-start | bytes 7372808 | tf_op jit(solution)/shard_map/ppermute | solution.py:162
  2134.5 41.5 %collective-permute-start.28 = (bf16[1536,5120]{1,0:T(8,128)(2,1)}, bf16[1536,5120]{1,0:T(8,128)(2,1)}, u32[]{:S(2)}, u32[]{:S(2)}) collective-permute-start(bf16[1536,5120]{1,0:T(8,128)(2,1)} %convolution_convert_fusion.4), channel_id=1, source_target_pairs={{0,1},{1,0},{2,3},{3,2},{4,5},{5,4},{6,7},{7,6}} | collective-permute-start | bytes 47185928 | tf_op jit(solution)/shard_map/ppermute | solution.py:162
  2175.9 456.4 %all-gather.32.cloned.1.call-start = ((), (), s32[]{:S(2)}) async-start(), calls=%async_computation.15 | async-start | bytes 17694720 | tf_op jit(solution)/shard_map/all_gather | solution.py:224
  2182.7 82.5 %collective-permute-start.30 = (f32[96,5120]{1,0:T(8,128)}, f32[96,5120]{1,0:T(8,128)}, u32[]{:S(2)}, u32[]{:S(2)}) collective-permute-start(f32[96,5120]{1,0:T(8,128)} %get-tuple-element.108), channel_id=1, source_target_pairs={{0,2},{1,3},{2,0},{3,1},{4,6},{5,7},{6,4},{7,5}} | collective-permute-start | bytes 5898248 | tf_op jit(solution)/shard_map/ppermute | solution.py:162
  2183.8 82.8 %collective-permute-start.32 = (f32[96,5120]{1,0:T(8,128)}, f32[96,5120]{1,0:T(8,128)}, u32[]{:S(2)}, u32[]{:S(2)}) collective-permute-start(f32[96,5120]{1,0:T(8,128)} %get-tuple-element.107), channel_id=1, source_target_pairs={{0,4},{1,5},{2,6},{3,7},{4,0},{5,1},{6,2},{7,3}} | collective-permute-start | bytes 5898248 | tf_op jit(solution)/shard_map/ppermute | solution.py:162
  2237.7 111.7 %collective-permute-start.29 = (f32[96,5120]{1,0:T(8,128)S(1)}, f32[96,5120]{1,0:T(8,128)S(1)}, u32[]{:S(2)}, u32[]{:S(2)}) collective-permute-start(f32[96,5120]{1,0:T(8,128)S(1)} %copy-done.20), channel_id=1, source_target_pairs={{0,2},{1,3},{2,0},{3,1},{4,6},{5,7},{6,4},{7,5}} | collective-permute-start | bytes 5898248 | tf_op jit(solution)/shard_map/ppermute | solution.py:162
  2238.8 111.3 %collective-permute-start.34 = (f32[96,5120]{1,0:T(8,128)S(1)}, f32[96,5120]{1,0:T(8,128)S(1)}, u32[]{:S(2)}, u32[]{:S(2)}) collective-permute-start(f32[96,5120]{1,0:T(8,128)S(1)} %get-tuple-element.106), channel_id=1, source_target_pairs={{0,4},{1,5},{2,6},{3,7},{4,0},{5,1},{6,2},{7,3}} | collective-permute-start | bytes 5898248 | tf_op jit(solution)/shard_map/ppermute | solution.py:162
  2270.6 119.5 %collective-permute-start.31 = (f32[96,5120]{1,0:T(8,128)S(1)}, f32[96,5120]{1,0:T(8,128)S(1)}, u32[]{:S(2)}, u32[]{:S(2)}) collective-permute-start(f32[96,5120]{1,0:T(8,128)S(1)} %get-tuple-element.109), channel_id=1, source_target_pairs={{0,4},{1,5},{2,6},{3,7},{4,0},{5,1},{6,2},{7,3}} | collective-permute-start | bytes 5898248 | tf_op jit(solution)/shard_map/ppermute | solution.py:162
  2272.1 118.1 %collective-permute-start.33 = (f32[96,5120]{1,0:T(8,128)S(1)}, f32[96,5120]{1,0:T(8,128)S(1)}, u32[]{:S(2)}, u32[]{:S(2)}) collective-permute-start(f32[96,5120]{1,0:T(8,128)S(1)} %get-tuple-element.110), channel_id=1, source_target_pairs={{0,2},{1,3},{2,0},{3,1},{4,6},{5,7},{6,4},{7,5}} | collective-permute-start | bytes 5898248 | tf_op jit(solution)/shard_map/ppermute | solution.py:162
  2395.2 250.0 %all-gather.24.cloned.1.call-start = ((), (), s32[]{:S(2)}) async-start(), calls=%async_computation.11 | async-start | bytes 13271040 | tf_op jit(solution)/shard_map/all_gather | solution.py:224
  2472.9 35.5 %collective-permute-start.16 = (f32[72,5120]{1,0:T(8,128)}, f32[72,5120]{1,0:T(8,128)}, u32[]{:S(2)}, u32[]{:S(2)}) collective-permute-start(f32[72,5120]{1,0:T(8,128)} %get-tuple-element.116), channel_id=1, source_target_pairs={{0,2},{1,3},{2,0},{3,1},{4,6},{5,7},{6,4},{7,5}} | collective-permute-start | bytes 4423688 | tf_op jit(solution)/shard_map/ppermute | solution.py:162
  2473.2 35.5 %collective-permute-start.18 = (f32[72,5120]{1,0:T(8,128)}, f32[72,5120]{1,0:T(8,128)}, u32[]{:S(2)}, u32[]{:S(2)}) collective-permute-start(f32[72,5120]{1,0:T(8,128)} %get-tuple-element.115), channel_id=1, source_target_pairs={{0,4},{1,5},{2,6},{3,7},{4,0},{5,1},{6,2},{7,3}} | collective-permute-start | bytes 4423688 | tf_op jit(solution)/shard_map/ppermute | solution.py:162
  2474.2 65.7 %collective-permute-start.15 = (f32[72,5120]{1,0:T(8,128)}, f32[72,5120]{1,0:T(8,128)}, u32[]{:S(2)}, u32[]{:S(2)}) collective-permute-start(f32[72,5120]{1,0:T(8,128)} %get-tuple-element.113), channel_id=1, source_target_pairs={{0,2},{1,3},{2,0},{3,1},{4,6},{5,7},{6,4},{7,5}} | collective-permute-start | bytes 4423688 | tf_op jit(solution)/shard_map/ppermute | solution.py:162
  2476.0 64.3 %collective-permute-start.20 = (f32[72,5120]{1,0:T(8,128)S(1)}, f32[72,5120]{1,0:T(8,128)}, u32[]{:S(2)}, u32[]{:S(2)}) collective-permute-start(f32[72,5120]{1,0:T(8,128)S(1)} %get-tuple-element.114), channel_id=1, source_target_pairs={{0,4},{1,5},{2,6},{3,7},{4,0},{5,1},{6,2},{7,3}} | collective-permute-start | bytes 4423688 | tf_op jit(solution)/shard_map/ppermute | solution.py:162
  2513.5 57.3 %collective-permute-start.17 = (f32[72,5120]{1,0:T(8,128)}, f32[72,5120]{1,0:T(8,128)}, u32[]{:S(2)}, u32[]{:S(2)}) collective-permute-start(f32[72,5120]{1,0:T(8,128)} %get-tuple-element.117), channel_id=1, source_target_pairs={{0,4},{1,5},{2,6},{3,7},{4,0},{5,1},{6,2},{7,3}} | collective-permute-start | bytes 4423688 | tf_op jit(solution)/shard_map/ppermute | solution.py:162
  2514.6 56.3 %collective-permute-start.19 = (f32[72,5120]{1,0:T(8,128)}, f32[72,5120]{1,0:T(8,128)}, u32[]{:S(2)}, u32[]{:S(2)}) collective-permute-start(f32[72,5120]{1,0:T(8,128)} %get-tuple-element.118), channel_id=1, source_target_pairs={{0,2},{1,3},{2,0},{3,1},{4,6},{5,7},{6,4},{7,5}} | collective-permute-start | bytes 4423688 | tf_op jit(solution)/shard_map/ppermute | solution.py:162
  (43 other events, 694.1 us)
Sparse Core Ops, SparseCore 0:
  14.7 264.8 all-gather.11
  353.2 140.3 all-gather.17
  495.5 112.9 all-gather.27
  859.6 173.2 all-gather.15
  1146.6 113.2 all-gather.19
  1411.1 140.5 all-gather.25
  1682.5 112.9 all-gather.29
  1909.5 63.0 all-gather.13
  2176.0 176.3 all-gather.21
  2395.3 79.8 all-gather.31
  2576.8 63.8 all-gather.23

commit v3 on v2

--- a/solution.py
+++ b/solution.py
@@ -10,7 +10,7 @@
 
 EPS = 1e-5
 ROPE_BASE = 10000.0
-CHUNKS = (6, 6, 5, 4, 3)
+CHUNKS = (4, 6, 6, 5, 3)
 PLACE_ROWS = 128
 Q_BLOCK = 128
 COL_TILE = 512
@@ -148,7 +148,7 @@
         out_specs=pl.BlockSpec((PLACE_ROWS, width), lambda i: (start // PLACE_ROWS + i, 0)),
         out_shape=jax.ShapeDtypeStruct((total_rows, width), jnp.bfloat16),
         input_output_aliases={} if y is None else {1: 0},
-        compiler_params=pltpu.CompilerParams(vmem_limit_bytes=16 * 1024 * 1024),
+        compiler_params=pltpu.CompilerParams(vmem_limit_bytes=60 * 1024 * 1024),
         cost_estimate=pl.CostEstimate(flops=rows * width, bytes_accessed=4 * rows * width, transcendentals=0),
         name="place",
     )(*operands)
@@ -206,7 +206,8 @@
             received.append(lax.all_to_all(attended[-1][0].reshape(tp_size, count * seq_len // tp_size, -1), "tp", 0, 0, tiled=True))
         new_keys = [keys for _, keys, _ in attended]
         new_values = [values for _, _, values in attended]
-        w_out_all, new_keys = lax.optimization_barrier((w_out_all, new_keys))
+        w_out_all, early_keys = lax.optimization_barrier((w_out_all, new_keys[:last]))
+        new_keys = early_keys + new_keys[last:]
         for index, (first, count) in enumerate(zip(starts, CHUNKS)):
             start_row = first * seq_len
             rows = count * seq_len // tp_size
@@ -218,8 +219,7 @@
             gated = (jax.nn.silu(gate_pre) * up_pre).astype(jnp.bfloat16)
             mlp_part = jnp.dot(gated, w_down, preferred_element_type=jnp.float32).astype(jnp.bfloat16)
             if index >= 2:
-                mlp_part, settled = lax.optimization_barrier((mlp_part, gathered[index - 2]))
-                y = settle(y, settled, index - 2)
+                y = settle(y, gathered[index - 2], index - 2)
             out_rows = sum_partials(mlp_part, hidden)
             gathered.append(lax.all_gather(out_rows, "tp", axis=0, tiled=True))
         for index in (last - 1, last):

time: 2670 us -> 2660 us (level)
  Pallas kernels: 467 us -> 519 us
  local copies, waits for them, and re-layouts: 73.7 us -> 46 us
    all_to_all x4, waiting for transfers between devices: 85.1 us -> 138 us  [layer_shard(): lax.all_to_all(attended[-1][0].reshape(tp_size, count * seq_len // tp_siz...]
    pallas_call x5, Pallas kernels: 44.2 us -> 91.5 us  [place(): pl.pallas_call(place_kernel, grid=(rows // PLACE_ROWS,), in_specs=[pl.Blo...]
    all_gather x5, waiting for transfers between devices: 40.1 us -> 0.02 us  [layer_shard(): normed_all = lax.all_gather(normed, 'tp', axis=0, tiled=True)]
    unnamed x93 -> x73, local copies, waits for them, and re-layouts: 54.2 us -> 25.9 us
    ppermute x35, waiting for transfers between devices: 543 us -> 516 us  [swap(): lax.ppermute(value, 'tp', [(index, index ^ bit) for index in range(tp_siz...]
  transfers between devices with their start and end apart: 50 -> 50, of which waited for: 22 -> 21; matrix products, arithmetic and copies ran while one was open for 51% -> 51% of each run, Pallas kernels for 16% -> 18%
where the time goes in v3:
time: 2660 us; the launch traced here: 2650 us
  matrix products  1210 us (45%)
  waiting for transfers between devices  653 us (25%)
  Pallas kernels  519 us (20%)
  other arithmetic  116 us (4%)
  blocking collectives  50 us (2%)
  local copies, waits for them, and re-layouts  46 us (2%)
  starting transfers between devices  41.8 us (2%)
    ppermute x35, waiting for transfers between devices, swap(): lax.ppermute(value, 'tp', [(index, index ^ bit) for index in range(tp_siz...  516 us
    dot_general x5, matrix products, layer_shard(): up_pre = jnp.dot(normed_all, w_up, preferred_element_type=jnp.float32)  425 us
    dot_general x5, matrix products, layer_shard(): gate_pre = jnp.dot(normed_all, w_gate, preferred_element_type=jnp.float32)  395 us
    dot_general x5, matrix products, layer_shard(): jnp.dot(gated, w_down, preferred_element_type=jnp.float32)  387 us
    pallas_call x5, Pallas kernels, attend(): pl.pallas_call(functools.partial(attend_kernel, first), grid_spec=grid_sp...  293 us
    all_to_all x4, waiting for transfers between devices, layer_shard(): lax.all_to_all(attended[-1][0].reshape(tp_size, count * seq_len // tp_siz...  138 us
    pallas_call x5, Pallas kernels, project(): pl.pallas_call(project_kernel, grid=(width // COL_TILE,), in_specs=[pl.Bl...  135 us
    pallas_call x5, Pallas kernels, place(): pl.pallas_call(place_kernel, grid=(rows // PLACE_ROWS,), in_specs=[pl.Blo...  91.5 us
  transfers between devices with their start and end apart: 50, of which 21 were waited for; matrix products, arithmetic and copies ran while one was open for 51% of the time, Pallas kernels for 18%

profile of v3, /device:TPU:0, one launch (start us, length us, event | category | flops | bytes accessed | tf_op | source)
XLA Modules:
  0.0 2649.6 jit_solution(8197637328208570993)
XLA Ops:
  20.5 52.6 %attend.6 = (bf16[4,384,640]{2,1,0:T(8,128)(2,1)}, bf16[4,384,128]{2,1,0:T(8,128)(2,1)}, bf16[4,384,128]{2,1,0:T(8,128)(2,1)}) custom-call(s32[24]{0:T(128)} %lens_ref.9, bf16[24,384,5120]{2,1,0:T(8,128)(2,1)} %x_ref.9, bf16[5120,640]{1,0:T(8,128)(2,1)} %wq_ref.9, bf16[5120,256]{1,0:T(8,128)(2,1)} %copy-done.12, bf16[1,5120]{1,0:T(2,128)(2,1)} %broadcast_in_dim.52.gain_ref, ...), custom_call_target="tpu_custom_call" | custom-call | flops 14092861440 | bytes 17694720 | tf_op jit(solution)/shard_map/attend/pallas_call | solution.py:91
  77.2 70.2 %attend.7 = (bf16[6,384,640]{2,1,0:T(8,128)(2,1)}, bf16[6,384,128]{2,1,0:T(8,128)(2,1)}, bf16[6,384,128]{2,1,0:T(8,128)(2,1)}) custom-call(s32[24]{0:T(128)} %lens_ref.9, bf16[24,384,5120]{2,1,0:T(8,128)(2,1)} %x_ref.9, bf16[5120,640]{1,0:T(8,128)(2,1)} %wq_ref.9, bf16[5120,256]{1,0:T(8,128)(2,1)} %copy-done.12, bf16[1,5120]{1,0:T(2,128)(2,1)} %broadcast_in_dim.52.gain_ref, ...), custom_call_target="tpu_custom_call" | custom-call | flops 21139292160 | bytes 26542080 | tf_op jit(solution)/shard_map/attend/pallas_call | solution.py:91
  147.4 70.2 %attend.8 = (bf16[6,384,640]{2,1,0:T(8,128)(2,1)}, bf16[6,384,128]{2,1,0:T(8,128)(2,1)}, bf16[6,384,128]{2,1,0:T(8,128)(2,1)}) custom-call(s32[24]{0:T(128)} %lens_ref.9, bf16[24,384,5120]{2,1,0:T(8,128)(2,1)} %x_ref.9, bf16[5120,640]{1,0:T(8,128)(2,1)} %wq_ref.9, bf16[5120,256]{1,0:T(8,128)(2,1)} %copy-done.12, bf16[1,5120]{1,0:T(2,128)(2,1)} %broadcast_in_dim.52.gain_ref, ...), custom_call_target="tpu_custom_call" | custom-call | flops 21139292160 | bytes 26542080 | tf_op jit(solution)/shard_map/attend/pallas_call | solution.py:91
  220.7 59.8 %attend.9 = (bf16[5,384,640]{2,1,0:T(8,128)(2,1)}, bf16[5,384,128]{2,1,0:T(8,128)(2,1)}, bf16[5,384,128]{2,1,0:T(8,128)(2,1)}) custom-call(s32[24]{0:T(128)} %lens_ref.9, bf16[24,384,5120]{2,1,0:T(8,128)(2,1)} %x_ref.9, bf16[5120,640]{1,0:T(8,128)(2,1)} %wq_ref.9, bf16[5120,256]{1,0:T(8,128)(2,1)} %copy-done.12, bf16[1,5120]{1,0:T(2,128)(2,1)} %broadcast_in_dim.52.gain_ref, ...), custom_call_target="tpu_custom_call" | custom-call | flops 17616076800 | bytes 22118400 | tf_op jit(solution)/shard_map/attend/pallas_call | solution.py:91
  280.5 23.4 project.9
  315.5 50.5 %all-to-all-done.3.o_ref = bf16[8,288,640]{2,1,0:T(8,128)(2,1)S(1)} async-done(((bf16[8,288,640]{2,1,0:T(8,128)(2,1)}), bf16[8,288,640]{2,1,0:T(8,128)(2,1)S(1)}, u32[]{:S(2)}, u32[]{:S(2)}) %all-to-all-start.3) | async-done | bytes 2949152 | tf_op jit(solution)/shard_map/all_to_all | solution.py:206
  367.6 31.9 %project.8 = (bf16[288,5120]{1,0:T(8,128)(2,1)S(1)}, bf16[288,5120]{1,0:T(8,128)(2,1)}) custom-call(bf16[8,288,640]{2,1,0:T(8,128)(2,1)} %copy-done.13, bf16[5120,5120]{1,0:T(8,128)(2,1)} %all-gather.12.cloned.1.call-done.w_ref, bf16[288,5120]{1,0:T(8,128)(2,1)} %get-tuple-element.63.x_ref, bf16[1,5120]{1,0:T(2,128)(2,1)S(1)} %broadcast_in_dim.57.gain_ref), custom_call_target="tpu_custom_call" | custom-call | flops 15099494400 | bytes 64225280 | tf_op jit(solution)/shard_map/project/pallas_call | solution.py:120
  403.0 50.0 %all_to_all.25.o_ref = bf16[8,288,640]{2,1,0:T(8,128)(2,1)} all-to-all(bf16[8,288,640]{2,1,0:T(8,128)(2,1)S(1)} %bitcast.49), channel_id=1, replica_groups=mesh['dp'=1,'tp'=8] {'tp'}, dimensions={0} | all-to-all | bytes 5898240 | tf_op jit(solution)/shard_map/all_to_all | solution.py:206
  453.0 29.7 %project.7 = (bf16[288,5120]{1,0:T(8,128)(2,1)S(1)}, bf16[288,5120]{1,0:T(8,128)(2,1)}) custom-call(bf16[8,288,640]{2,1,0:T(8,128)(2,1)} %all_to_all.25.o_ref, bf16[5120,5120]{1,0:T(8,128)(2,1)} %all-gather.12.cloned.1.call-done.w_ref, bf16[288,5120]{1,0:T(8,128)(2,1)} %get-tuple-element.64.x_ref, bf16[1,5120]{1,0:T(2,128)(2,1)S(1)} %broadcast_in_dim.57.gain_ref), custom_call_target="tpu_custom_call" | custom-call | flops 15099494400 | bytes 64225280 | tf_op jit(solution)/shard_map/project/pallas_call | solution.py:120
  490.0 53.7 %all-to-all-done.1.o_ref = bf16[8,240,640]{2,1,0:T(8,128)(2,1)S(1)} async-done(((bf16[8,240,640]{2,1,0:T(8,128)(2,1)}), bf16[8,240,640]{2,1,0:T(8,128)(2,1)S(1)}, u32[]{:S(2)}, u32[]{:S(2)}) %all-to-all-start.1) | async-done | bytes 2457632 | tf_op jit(solution)/shard_map/all_to_all | solution.py:206
  545.2 28.0 %project.6 = (bf16[240,5120]{1,0:T(8,128)(2,1)S(1)}, bf16[240,5120]{1,0:T(8,128)(2,1)}) custom-call(bf16[8,240,640]{2,1,0:T(8,128)(2,1)} %copy-done.14, bf16[5120,5120]{1,0:T(8,128)(2,1)} %all-gather.12.cloned.1.call-done.w_ref, bf16[240,5120]{1,0:T(8,128)(2,1)} %constant_dynamic-slice_fusion.3.x_ref, bf16[1,5120]{1,0:T(2,128)(2,1)S(1)} %broadcast_in_dim.57.gain_ref), custom_call_target="tpu_custom_call" | custom-call | flops 12582912000 | bytes 62259200 | tf_op jit(solution)/shard_map/project/pallas_call | solution.py:120
  574.7 39.9 %attend.5 = (bf16[3,384,640]{2,1,0:T(8,128)(2,1)}, bf16[3,384,128]{2,1,0:T(8,128)(2,1)}, bf16[3,384,128]{2,1,0:T(8,128)(2,1)}) custom-call(s32[24]{0:T(128)} %lens_ref.9, bf16[24,384,5120]{2,1,0:T(8,128)(2,1)} %x_ref.9, bf16[5120,640]{1,0:T(8,128)(2,1)} %wq_ref.9, bf16[5120,256]{1,0:T(8,128)(2,1)} %copy-done.12, bf16[1,5120]{1,0:T(2,128)(2,1)} %broadcast_in_dim.52.gain_ref, ...), custom_call_target="tpu_custom_call" | custom-call | flops 10569646080 | bytes 13271040 | tf_op jit(solution)/shard_map/attend/pallas_call | solution.py:91
  618.5 33.5 %all-to-all-done.o_ref = bf16[8,144,640]{2,1,0:T(8,128)(2,1)S(1)} async-done(((bf16[8,144,640]{2,1,0:T(8,128)(2,1)}), bf16[8,144,640]{2,1,0:T(8,128)(2,1)S(1)}, u32[]{:S(2)}, u32[]{:S(2)}) %all-to-all-start) | async-done | bytes 1474592 | tf_op jit(solution)/shard_map/all_to_all | solution.py:206
  652.0 22.0 project.5
  676.4 67.4 %fusion.5 = f32[1536,3456]{1,0:T(8,128)} fusion(bf16[1536,5120]{1,0:T(8,128)(2,1)} %all-gather.30.cloned.1.call-done, bf16[5120,3456]{1,0:T(8,128)(2,1)} %param.19), kind=kOutput, calls=%fused_computation.86 | convolution fusion | flops 54358179840 | bytes 72351744 | tf_op jit(solution)/shard_map/dot_general | solution.py:217
  743.8 72.2 %multiply_convert_fusion.3 = bf16[1536,3456]{1,0:T(8,128)(2,1)S(1)} fusion(f32[1536,3456]{1,0:T(8,128)} %fusion.5, bf16[1536,5120]{1,0:T(8,128)(2,1)} %all-gather.30.cloned.1.call-done, bf16[5120,3456]{1,0:T(8,128)(2,1)} %param.20), kind=kOutput, calls=%fused_computation.5 | convolution fusion | flops 54390030336 | bytes 82968576 | tf_op jit(solution)/shard_map/dot_general | solution.py:218
  816.0 63.2 %convolution_convert_fusion.4 = bf16[1536,5120]{1,0:T(8,128)(2,1)} fusion(bf16[1536,3456]{1,0:T(8,128)(2,1)S(1)} %multiply_convert_fusion.3, bf16[3456,5120]{1,0:T(8,128)(2,1)} %param.21), kind=kOutput, calls=%fused_computation.9 | convolution fusion | flops 54366044160 | bytes 61734912 | tf_op jit(solution)/shard_map/dot_general | solution.py:220
  879.2 97.0 %fusion.4 = f32[2304,3456]{1,0:T(8,128)} fusion(bf16[2304,5120]{1,0:T(8,128)(2,1)} %all-gather.26.cloned.1.call-done, bf16[5120,3456]{1,0:T(8,128)(2,1)} %param.19), kind=kOutput, calls=%fused_computation.85 | convolution fusion | flops 81537269760 | bytes 90832896 | tf_op jit(solution)/shard_map/dot_general | solution.py:217
  976.2 104.8 %multiply_convert_fusion = bf16[2304,3456]{1,0:T(8,128)(2,1)} fusion(f32[2304,3456]{1,0:T(8,128)} %fusion.4, bf16[2304,5120]{1,0:T(8,128)(2,1)} %all-gather.26.cloned.1.call-done, bf16[5120,3456]{1,0:T(8,128)(2,1)} %param.20), kind=kOutput, calls=%fused_computation | convolution fusion | flops 81585045504 | bytes 106758144 | tf_op jit(solution)/shard_map/dot_general | solution.py:218
  1081.0 94.8 %convolution_convert_fusion = bf16[2304,5120]{1,0:T(8,128)(2,1)} fusion(bf16[2304,3456]{1,0:T(8,128)(2,1)} %multiply_convert_fusion, bf16[3456,5120]{1,0:T(8,128)(2,1)} %param.21), kind=kOutput, calls=%fused_computation.2 | convolution fusion | flops 81549066240 | bytes 74907648 | tf_op jit(solution)/shard_map/dot_general | solution.py:220
  1185.8 97.0 %fusion.3 = f32[2304,3456]{1,0:T(8,128)} fusion(bf16[2304,5120]{1,0:T(8,128)(2,1)} %all-gather.22.cloned.1.call-done, bf16[5120,3456]{1,0:T(8,128)(2,1)} %param.19), kind=kOutput, calls=%fused_computation.84 | convolution fusion | flops 81537269760 | bytes 90832896 | tf_op jit(solution)/shard_map/dot_general | solution.py:217
  1292.8 104.8 %multiply_convert_fusion.1 = bf16[2304,3456]{1,0:T(8,128)(2,1)} fusion(f32[2304,3456]{1,0:T(8,128)} %fusion.3, bf16[2304,5120]{1,0:T(8,128)(2,1)} %all-gather.22.cloned.1.call-done, bf16[5120,3456]{1,0:T(8,128)(2,1)} %param.20), kind=kOutput, calls=%fused_computation.1 | convolution fusion | flops 81585045504 | bytes 106758144 | tf_op jit(solution)/shard_map/dot_general | solution.py:218
  1405.1 96.5 %convolution_convert_fusion.1 = bf16[2304,5120]{1,0:T(8,128)(2,1)} fusion(bf16[2304,3456]{1,0:T(8,128)(2,1)} %multiply_convert_fusion.1, bf16[3456,5120]{1,0:T(8,128)(2,1)} %param.21), kind=kOutput, calls=%fused_computation.3 | convolution fusion | flops 81549066240 | bytes 74907648 | tf_op jit(solution)/shard_map/dot_general | solution.py:220
  1501.7 9.8 convert_add_fusion.3
  1515.5 63.0 %collective-permute-done.23 = f32[144,5120]{1,0:T(8,128)} collective-permute-done((f32[144,5120]{1,0:T(8,128)}, f32[144,5120]{1,0:T(8,128)}, u32[]{:S(2)}, u32[]{:S(2)}) %collective-permute-start.23) | collective-permute-done | bytes 2949152 | tf_op jit(solution)/shard_map/ppermute | solution.py:162
  1588.9 52.8 %collective-permute-done.22 = f32[144,5120]{1,0:T(8,128)} collective-permute-done((f32[144,5120]{1,0:T(8,128)}, f32[144,5120]{1,0:T(8,128)}, u32[]{:S(2)}, u32[]{:S(2)}) %collective-permute-start.22) | collective-permute-done | bytes 2949152 | tf_op jit(solution)/shard_map/ppermute | solution.py:162
  1642.1 62.4 %collective-permute-done.24 = f32[144,5120]{1,0:T(8,128)} collective-permute-done((f32[144,5120]{1,0:T(8,128)}, f32[144,5120]{1,0:T(8,128)}, u32[]{:S(2)}, u32[]{:S(2)}) %collective-permute-start.24) | collective-permute-done | bytes 2949152 | tf_op jit(solution)/shard_map/ppermute | solution.py:162
  1714.0 10.9 convert_add_fusion.7
  1726.5 82.7 %fusion.2 = f32[1920,3456]{1,0:T(8,128)} fusion(bf16[1920,5120]{1,0:T(8,128)(2,1)} %all-gather.18.cloned.1.call-done, bf16[5120,3456]{1,0:T(8,128)(2,1)} %param.19), kind=kOutput, calls=%fused_computation.83 | convolution fusion | flops 67947724800 | bytes 81592320 | tf_op jit(solution)/shard_map/dot_general | solution.py:217
  1811.7 36.9 %collective-permute-done.16 = f32[144,5120]{1,0:T(8,128)} collective-permute-done((f32[144,5120]{1,0:T(8,128)}, f32[144,5120]{1,0:T(8,128)}, u32[]{:S(2)}, u32[]{:S(2)}) %collective-permute-start.16) | collective-permute-done | bytes 2949152 | tf_op jit(solution)/shard_map/ppermute | solution.py:162
  1859.9 87.9 %multiply_convert_fusion.2 = bf16[1920,3456]{1,0:T(8,128)(2,1)} fusion(f32[1920,3456]{1,0:T(8,128)} %fusion.2, bf16[1920,5120]{1,0:T(8,128)(2,1)} %all-gather.18.cloned.1.call-done, bf16[5120,3456]{1,0:T(8,128)(2,1)} %param.20), kind=kOutput, calls=%fused_computation.4 | convolution fusion | flops 67987537920 | bytes 94863360 | tf_op jit(solution)/shard_map/dot_general | solution.py:218
  1947.8 61.0 %collective-permute-done.17 = f32[144,5120]{1,0:T(8,128)} collective-permute-done((f32[144,5120]{1,0:T(8,128)}, f32[144,5120]{1,0:T(8,128)}, u32[]{:S(2)}, u32[]{:S(2)}) %collective-permute-start.17) | collective-permute-done | bytes 2949152 | tf_op jit(solution)/shard_map/ppermute | solution.py:162
  2017.8 83.9 %convolution_convert_fusion.2 = bf16[1920,5120]{1,0:T(8,128)(2,1)} fusion(bf16[1920,3456]{1,0:T(8,128)(2,1)} %multiply_convert_fusion.2, bf16[3456,5120]{1,0:T(8,128)(2,1)} %param.21), kind=kOutput, calls=%fused_computation.7 | convolution fusion | flops 67957555200 | bytes 68321280 | tf_op jit(solution)/shard_map/dot_general | solution.py:220
  2101.8 33.8 %collective-permute-done.7 = bf16[1920,5120]{1,0:T(8,128)(2,1)} collective-permute-done((bf16[1920,5120]{1,0:T(8,128)(2,1)}, bf16[1920,5120]{1,0:T(8,128)(2,1)}, u32[]{:S(2)}, u32[]{:S(2)}) %collective-permute-start.7) | collective-permute-done | bytes 19660832 | tf_op jit(solution)/shard_map/ppermute | solution.py:162
  2147.3 52.5 %collective-permute-done.9 = f32[120,5120]{1,0:T(8,128)} collective-permute-done((f32[120,5120]{1,0:T(8,128)}, f32[120,5120]{1,0:T(8,128)}, u32[]{:S(2)}, u32[]{:S(2)}) %collective-permute-start.9) | collective-permute-done | bytes 2457632 | tf_op jit(solution)/shard_map/ppermute | solution.py:162
  2209.4 51.4 %fusion.1 = f32[1152,3456]{1,0:T(8,128)} fusion(bf16[1152,5120]{1,0:T(8,128)(2,1)} %all-gather.14.cloned.1.call-done, bf16[5120,3456]{1,0:T(8,128)(2,1)} %param.19), kind=kOutput, calls=%fused_computation.82 | convolution fusion | flops 40768634880 | bytes 63111168 | tf_op jit(solution)/shard_map/dot_general | solution.py:217
  2260.8 44.3 %collective-permute-done.10 = f32[120,5120]{1,0:T(8,128)} collective-permute-done((f32[120,5120]{1,0:T(8,128)}, f32[120,5120]{1,0:T(8,128)}, u32[]{:S(2)}, u32[]{:S(2)}) %collective-permute-start.10) | collective-permute-done | bytes 2457632 | tf_op jit(solution)/shard_map/ppermute | solution.py:162
  2313.8 55.5 %fusion = bf16[1152,3456]{1,0:T(8,128)(2,1)S(1)} fusion(bf16[1152,5120]{1,0:T(8,128)(2,1)} %all-gather.14.cloned.1.call-done, bf16[5120,3456]{1,0:T(8,128)(2,1)} %param.20, f32[1152,3456]{1,0:T(8,128)} %fusion.1), kind=kOutput, calls=%fused_computation.10 | convolution fusion | flops 40792522752 | bytes 71073792 | tf_op jit(solution)/shard_map/dot_general | solution.py:218
  2369.3 49.0 %convolution_convert_fusion.3 = bf16[1152,5120]{1,0:T(8,128)(2,1)} fusion(bf16[1152,3456]{1,0:T(8,128)(2,1)S(1)} %fusion, bf16[3456,5120]{1,0:T(8,128)(2,1)} %param.21), kind=kOutput, calls=%fused_computation.8 | convolution fusion | flops 40774533120 | bytes 55148544 | tf_op jit(solution)/shard_map/dot_general | solution.py:220
  2418.4 18.3 collective-permute-done
  2445.9 31.4 %collective-permute-done.2 = f32[72,5120]{1,0:T(8,128)} collective-permute-done((f32[72,5120]{1,0:T(8,128)}, f32[72,5120]{1,0:T(8,128)}, u32[]{:S(2)}, u32[]{:S(2)}) %collective-permute-start.2) | collective-permute-done | bytes 1474592 | tf_op jit(solution)/shard_map/ppermute | solution.py:162
  2484.2 24.8 collective-permute-done.1
  2509.3 30.5 %collective-permute-done.3 = f32[72,5120]{1,0:T(8,128)} collective-permute-done((f32[72,5120]{1,0:T(8,128)}, f32[72,5120]{1,0:T(8,128)}, u32[]{:S(2)}, u32[]{:S(2)}) %collective-permute-start.3) | collective-permute-done | bytes 1474592 | tf_op jit(solution)/shard_map/ppermute | solution.py:162
  2551.2 15.1 place.5.refs_0_
  2566.4 22.4 place.6.refs_0_
  2588.8 22.3 place.7.refs_0_
  2611.2 19.4 place.8.refs_0_
  2630.6 12.2 place.9
  (208 shorter events, 187.3 us)
Async XLA Ops:
  7.2 273.4 %all-gather.12.cloned.1.call-start = ((), (), s32[]{:S(2)}) async-start(), calls=%async_computation.5 | async-start | bytes 58982400 | tf_op jit(solution)/shard_map/all_gather | solution.py:188
  73.1 207.4 %all-to-all-start.4 = ((bf16[8,192,640]{2,1,0:T(8,128)(2,1)}), bf16[8,192,640]{2,1,0:T(8,128)(2,1)S(1)}, u32[]{:S(2)}, u32[]{:S(2)}) async-start(bf16[8,192,640]{2,1,0:T(8,128)(2,1)} %bitcast.52), calls=%async_computation.4 | async-start | bytes 3932160 | tf_op jit(solution)/shard_map/all_to_all | solution.py:206
  77.0 599.4 %all-gather.30.cloned.1.call-start = ((), (), s32[]{:S(2)}) async-start(), calls=%async_computation.14 | async-start | bytes 17694720 | tf_op jit(solution)/shard_map/all_gather | solution.py:216
  306.5 59.5 %all-to-all-start.3 = ((bf16[8,288,640]{2,1,0:T(8,128)(2,1)}), bf16[8,288,640]{2,1,0:T(8,128)(2,1)S(1)}, u32[]{:S(2)}, u32[]{:S(2)}) async-start(bf16[8,288,640]{2,1,0:T(8,128)(2,1)} %bitcast.50), calls=%async_computation.3 | async-start | bytes 5898240 | tf_op jit(solution)/shard_map/all_to_all | solution.py:206
  309.2 569.9 %all-gather.26.cloned.1.call-start = ((), (), s32[]{:S(2)}) async-start(), calls=%async_computation.12 | async-start | bytes 26542080 | tf_op jit(solution)/shard_map/all_gather | solution.py:216
  401.2 784.6 %all-gather.22.cloned.1.call-start = ((), (), s32[]{:S(2)}) async-start(), calls=%async_computation.10 | async-start | bytes 26542080 | tf_op jit(solution)/shard_map/all_gather | solution.py:216
  484.3 59.5 %all-to-all-start.1 = ((bf16[8,240,640]{2,1,0:T(8,128)(2,1)}), bf16[8,240,640]{2,1,0:T(8,128)(2,1)S(1)}, u32[]{:S(2)}, u32[]{:S(2)}) async-start(bf16[8,240,640]{2,1,0:T(8,128)(2,1)} %bitcast.51), calls=%async_computation.1 | async-start | bytes 4915200 | tf_op jit(solution)/shard_map/all_to_all | solution.py:206
  486.6 1239.9 %all-gather.18.cloned.1.call-start = ((), (), s32[]{:S(2)}) async-start(), calls=%async_computation.8 | async-start | bytes 22118400 | tf_op jit(solution)/shard_map/all_gather | solution.py:216
  614.6 37.4 %all-to-all-start = ((bf16[8,144,640]{2,1,0:T(8,128)(2,1)}), bf16[8,144,640]{2,1,0:T(8,128)(2,1)S(1)}, u32[]{:S(2)}, u32[]{:S(2)}) async-start(bf16[8,144,640]{2,1,0:T(8,128)(2,1)} %bitcast.53), calls=%async_computation | async-start | bytes 2949120 | tf_op jit(solution)/shard_map/all_to_all | solution.py:206
  616.9 1592.5 %all-gather.14.cloned.1.call-start = ((), (), s32[]{:S(2)}) async-start(), calls=%async_computation.6 | async-start | bytes 13271040 | tf_op jit(solution)/shard_map/all_gather | solution.py:216
  676.4 1874.9 %all-gather.32.cloned.1.call-start = ((), (), s32[]{:S(2)}) async-start(), calls=%async_computation.15 | async-start | bytes 17694720 | tf_op jit(solution)/shard_map/all_gather | solution.py:224
  879.1 297.1 %collective-permute-start.28 = (bf16[1536,5120]{1,0:T(8,128)(2,1)}, bf16[1536,5120]{1,0:T(8,128)(2,1)}, u32[]{:S(2)}, u32[]{:S(2)}) collective-permute-start(bf16[1536,5120]{1,0:T(8,128)(2,1)} %convolution_convert_fusion.4), channel_id=1, source_target_pairs={{0,1},{1,0},{2,3},{3,2},{4,5},{5,4},{6,7},{7,6}} | collective-permute-start | bytes 47185928 | tf_op jit(solution)/shard_map/ppermute | solution.py:162
  1175.8 325.9 %collective-permute-start.21 = (bf16[2304,5120]{1,0:T(8,128)(2,1)}, bf16[2304,5120]{1,0:T(8,128)(2,1)}, u32[]{:S(2)}, u32[]{:S(2)}) collective-permute-start(bf16[2304,5120]{1,0:T(8,128)(2,1)} %convolution_convert_fusion), channel_id=1, source_target_pairs={{0,1},{1,0},{2,3},{3,2},{4,5},{5,4},{6,7},{7,6}} | collective-permute-start | bytes 70778888 | tf_op jit(solution)/shard_map/ppermute | solution.py:162
  1183.3 101.0 %collective-permute-start.30 = (f32[96,5120]{1,0:T(8,128)}, f32[96,5120]{1,0:T(8,128)}, u32[]{:S(2)}, u32[]{:S(2)}) collective-permute-start(f32[96,5120]{1,0:T(8,128)} %get-tuple-element.94), channel_id=1, source_target_pairs={{0,2},{1,3},{2,0},{3,1},{4,6},{5,7},{6,4},{7,5}} | collective-permute-start | bytes 5898248 | tf_op jit(solution)/shard_map/ppermute | solution.py:162
  1184.0 100.3 %collective-permute-start.32 = (f32[96,5120]{1,0:T(8,128)}, f32[96,5120]{1,0:T(8,128)}, u32[]{:S(2)}, u32[]{:S(2)}) collective-permute-start(f32[96,5120]{1,0:T(8,128)} %get-tuple-element.93), channel_id=1, source_target_pairs={{0,4},{1,5},{2,6},{3,7},{4,0},{5,1},{6,2},{7,3}} | collective-permute-start | bytes 5898248 | tf_op jit(solution)/shard_map/ppermute | solution.py:162
  1282.7 115.0 %collective-permute-start.29 = (f32[96,5120]{1,0:T(8,128)}, f32[96,5120]{1,0:T(8,128)}, u32[]{:S(2)}, u32[]{:S(2)}) collective-permute-start(f32[96,5120]{1,0:T(8,128)} %get-tuple-element.91), channel_id=1, source_target_pairs={{0,2},{1,3},{2,0},{3,1},{4,6},{5,7},{6,4},{7,5}} | collective-permute-start | bytes 5898248 | tf_op jit(solution)/shard_map/ppermute | solution.py:162
  1283.4 114.3 %collective-permute-start.34 = (f32[96,5120]{1,0:T(8,128)}, f32[96,5120]{1,0:T(8,128)}, u32[]{:S(2)}, u32[]{:S(2)}) collective-permute-start(f32[96,5120]{1,0:T(8,128)} %get-tuple-element.92), channel_id=1, source_target_pairs={{0,4},{1,5},{2,6},{3,7},{4,0},{5,1},{6,2},{7,3}} | collective-permute-start | bytes 5898248 | tf_op jit(solution)/shard_map/ppermute | solution.py:162
  1290.4 107.3 %collective-permute-start.31 = (f32[96,5120]{1,0:T(8,128)}, f32[96,5120]{1,0:T(8,128)}, u32[]{:S(2)}, u32[]{:S(2)}) collective-permute-start(f32[96,5120]{1,0:T(8,128)} %get-tuple-element.95), channel_id=1, source_target_pairs={{0,4},{1,5},{2,6},{3,7},{4,0},{5,1},{6,2},{7,3}} | collective-permute-start | bytes 5898248 | tf_op jit(solution)/shard_map/ppermute | solution.py:162
  1291.5 106.2 %collective-permute-start.33 = (f32[96,5120]{1,0:T(8,128)}, f32[96,5120]{1,0:T(8,128)}, u32[]{:S(2)}, u32[]{:S(2)}) collective-permute-start(f32[96,5120]{1,0:T(8,128)} %get-tuple-element.96), channel_id=1, source_target_pairs={{0,2},{1,3},{2,0},{3,1},{4,6},{5,7},{6,4},{7,5}} | collective-permute-start | bytes 5898248 | tf_op jit(solution)/shard_map/ppermute | solution.py:162
  1405.1 1161.3 %all-gather.28.cloned.1.call-start = ((), (), s32[]{:S(2)}) async-start(), calls=%async_computation.13 | async-start | bytes 26542080 | tf_op jit(solution)/shard_map/all_gather | solution.py:224
  1501.7 212.4 %collective-permute-start.14 = (bf16[2304,5120]{1,0:T(8,128)(2,1)}, bf16[2304,5120]{1,0:T(8,128)(2,1)}, u32[]{:S(2)}, u32[]{:S(2)}) collective-permute-start(bf16[2304,5120]{1,0:T(8,128)(2,1)} %convolution_convert_fusion.1), channel_id=1, source_target_pairs={{0,1},{1,0},{2,3},{3,2},{4,5},{5,4},{6,7},{7,6}} | collective-permute-start | bytes 70778888 | tf_op jit(solution)/shard_map/ppermute | solution.py:162
  1511.5 67.1 %collective-permute-start.23 = (f32[144,5120]{1,0:T(8,128)}, f32[144,5120]{1,0:T(8,128)}, u32[]{:S(2)}, u32[]{:S(2)}) collective-permute-start(f32[144,5120]{1,0:T(8,128)} %get-tuple-element.72), channel_id=1, source_target_pairs={{0,2},{1,3},{2,0},{3,1},{4,6},{5,7},{6,4},{7,5}} | collective-permute-start | bytes 8847368 | tf_op jit(solution)/shard_map/ppermute | solution.py:162
  1511.8 67.1 %collective-permute-start.25 = (f32[144,5120]{1,0:T(8,128)}, f32[144,5120]{1,0:T(8,128)}, u32[]{:S(2)}, u32[]{:S(2)}) collective-permute-start(f32[144,5120]{1,0:T(8,128)} %get-tuple-element.71), channel_id=1, source_target_pairs={{0,4},{1,5},{2,6},{3,7},{4,0},{5,1},{6,2},{7,3}} | collective-permute-start | bytes 8847368 | tf_op jit(solution)/shard_map/ppermute | solution.py:162
  1512.0 129.7 %collective-permute-start.22 = (f32[144,5120]{1,0:T(8,128)}, f32[144,5120]{1,0:T(8,128)}, u32[]{:S(2)}, u32[]{:S(2)}) collective-permute-start(f32[144,5120]{1,0:T(8,128)} %get-tuple-element.69), channel_id=1, source_target_pairs={{0,2},{1,3},{2,0},{3,1},{4,6},{5,7},{6,4},{7,5}} | collective-permute-start | bytes 8847368 | tf_op jit(solution)/shard_map/ppermute | solution.py:162
  1513.5 128.6 %collective-permute-start.27 = (f32[144,5120]{1,0:T(8,128)}, f32[144,5120]{1,0:T(8,128)}, u32[]{:S(2)}, u32[]{:S(2)}) collective-permute-start(f32[144,5120]{1,0:T(8,128)} %get-tuple-element.70), channel_id=1, source_target_pairs={{0,4},{1,5},{2,6},{3,7},{4,0},{5,1},{6,2},{7,3}} | collective-permute-start | bytes 8847368 | tf_op jit(solution)/shard_map/ppermute | solution.py:162
  1587.2 117.3 %collective-permute-start.24 = (f32[144,5120]{1,0:T(8,128)}, f32[144,5120]{1,0:T(8,128)}, u32[]{:S(2)}, u32[]{:S(2)}) collective-permute-start(f32[144,5120]{1,0:T(8,128)} %get-tuple-element.73), channel_id=1, source_target_pairs={{0,4},{1,5},{2,6},{3,7},{4,0},{5,1},{6,2},{7,3}} | collective-permute-start | bytes 8847368 | tf_op jit(solution)/shard_map/ppermute | solution.py:162
  1587.4 117.1 %collective-permute-start.26 = (f32[144,5120]{1,0:T(8,128)}, f32[144,5120]{1,0:T(8,128)}, u32[]{:S(2)}, u32[]{:S(2)}) collective-permute-start(f32[144,5120]{1,0:T(8,128)} %get-tuple-element.74), channel_id=1, source_target_pairs={{0,2},{1,3},{2,0},{3,1},{4,6},{5,7},{6,4},{7,5}} | collective-permute-start | bytes 8847368 | tf_op jit(solution)/shard_map/ppermute | solution.py:162
  1713.8 875.0 %all-gather.24.cloned.1.call-start = ((), (), s32[]{:S(2)}) async-start(), calls=%async_computation.11 | async-start | bytes 26542080 | tf_op jit(solution)/shard_map/all_gather | solution.py:224
  1725.0 123.7 %collective-permute-start.16 = (f32[144,5120]{1,0:T(8,128)}, f32[144,5120]{1,0:T(8,128)}, u32[]{:S(2)}, u32[]{:S(2)}) collective-permute-start(f32[144,5120]{1,0:T(8,128)} %get-tuple-element.78), channel_id=1, source_target_pairs={{0,2},{1,3},{2,0},{3,1},{4,6},{5,7},{6,4},{7,5}} | collective-permute-start | bytes 8847368 | tf_op jit(solution)/shard_map/ppermute | solution.py:162
  1726.4 123.3 %collective-permute-start.18 = (f32[144,5120]{1,0:T(8,128)}, f32[144,5120]{1,0:T(8,128)}, u32[]{:S(2)}, u32[]{:S(2)}) collective-permute-start(f32[144,5120]{1,0:T(8,128)} %get-tuple-element.77), channel_id=1, source_target_pairs={{0,4},{1,5},{2,6},{3,7},{4,0},{5,1},{6,2},{7,3}} | collective-permute-start | bytes 8847368 | tf_op jit(solution)/shard_map/ppermute | solution.py:162
  1809.2 138.6 %collective-permute-start.15 = (f32[144,5120]{1,0:T(8,128)}, f32[144,5120]{1,0:T(8,128)}, u32[]{:S(2)}, u32[]{:S(2)}) collective-permute-start(f32[144,5120]{1,0:T(8,128)} %get-tuple-element.75), channel_id=1, source_target_pairs={{0,2},{1,3},{2,0},{3,1},{4,6},{5,7},{6,4},{7,5}} | collective-permute-start | bytes 8847368 | tf_op jit(solution)/shard_map/ppermute | solution.py:162
  1809.7 138.1 %collective-permute-start.20 = (f32[144,5120]{1,0:T(8,128)}, f32[144,5120]{1,0:T(8,128)}, u32[]{:S(2)}, u32[]{:S(2)}) collective-permute-start(f32[144,5120]{1,0:T(8,128)} %get-tuple-element.76), channel_id=1, source_target_pairs={{0,4},{1,5},{2,6},{3,7},{4,0},{5,1},{6,2},{7,3}} | collective-permute-start | bytes 8847368 | tf_op jit(solution)/shard_map/ppermute | solution.py:162
  1858.1 150.8 %collective-permute-start.17 = (f32[144,5120]{1,0:T(8,128)}, f32[144,5120]{1,0:T(8,128)}, u32[]{:S(2)}, u32[]{:S(2)}) collective-permute-start(f32[144,5120]{1,0:T(8,128)} %get-tuple-element.79), channel_id=1, source_target_pairs={{0,4},{1,5},{2,6},{3,7},{4,0},{5,1},{6,2},{7,3}} | collective-permute-start | bytes 8847368 | tf_op jit(solution)/shard_map/ppermute | solution.py:162
  1858.2 150.6 %collective-permute-start.19 = (f32[144,5120]{1,0:T(8,128)}, f32[144,5120]{1,0:T(8,128)}, u32[]{:S(2)}, u32[]{:S(2)}) collective-permute-start(f32[144,5120]{1,0:T(8,128)} %get-tuple-element.80), channel_id=1, source_target_pairs={{0,2},{1,3},{2,0},{3,1},{4,6},{5,7},{6,4},{7,5}} | collective-permute-start | bytes 8847368 | tf_op jit(solution)/shard_map/ppermute | solution.py:162
  2017.8 593.4 %all-gather.20.cloned.1.call-start = ((), (), s32[]{:S(2)}) async-start(), calls=%async_computation.9 | async-start | bytes 22118400 | tf_op jit(solution)/shard_map/all_gather | solution.py:224
  2143.2 56.5 %collective-permute-start.9 = (f32[120,5120]{1,0:T(8,128)}, f32[120,5120]{1,0:T(8,128)}, u32[]{:S(2)}, u32[]{:S(2)}) collective-permute-start(f32[120,5120]{1,0:T(8,128)} %get-tuple-element.86), channel_id=1, source_target_pairs={{0,2},{1,3},{2,0},{3,1},{4,6},{5,7},{6,4},{7,5}} | collective-permute-start | bytes 7372808 | tf_op jit(solution)/shard_map/ppermute | solution.py:162
  2144.6 56.3 %collective-permute-start.11 = (f32[120,5120]{1,0:T(8,128)S(1)}, f32[120,5120]{1,0:T(8,128)}, u32[]{:S(2)}, u32[]{:S(2)}) collective-permute-start(f32[120,5120]{1,0:T(8,128)S(1)} %get-tuple-element.85), channel_id=1, source_target_pairs={{0,4},{1,5},{2,6},{3,7},{4,0},{5,1},{6,2},{7,3}} | collective-permute-start | bytes 7372808 | tf_op jit(solution)/shard_map/ppermute | solution.py:162
  2144.7 116.2 %collective-permute-start.8 = (f32[120,5120]{1,0:T(8,128)}, f32[120,5120]{1,0:T(8,128)}, u32[]{:S(2)}, u32[]{:S(2)}) collective-permute-start(f32[120,5120]{1,0:T(8,128)} %get-tuple-element.83), channel_id=1, source_target_pairs={{0,2},{1,3},{2,0},{3,1},{4,6},{5,7},{6,4},{7,5}} | collective-permute-start | bytes 7372808 | tf_op jit(solution)/shard_map/ppermute | solution.py:162
  2145.8 115.0 %collective-permute-start.13 = (f32[120,5120]{1,0:T(8,128)}, f32[120,5120]{1,0:T(8,128)}, u32[]{:S(2)}, u32[]{:S(2)}) collective-permute-start(f32[120,5120]{1,0:T(8,128)} %get-tuple-element.84), channel_id=1, source_target_pairs={{0,4},{1,5},{2,6},{3,7},{4,0},{5,1},{6,2},{7,3}} | collective-permute-start | bytes 7372808 | tf_op jit(solution)/shard_map/ppermute | solution.py:162
  2208.1 97.0 %collective-permute-start.10 = (f32[120,5120]{1,0:T(8,128)}, f32[120,5120]{1,0:T(8,128)}, u32[]{:S(2)}, u32[]{:S(2)}) collective-permute-start(f32[120,5120]{1,0:T(8,128)} %get-tuple-element.87), channel_id=1, source_target_pairs={{0,4},{1,5},{2,6},{3,7},{4,0},{5,1},{6,2},{7,3}} | collective-permute-start | bytes 7372808 | tf_op jit(solution)/shard_map/ppermute | solution.py:162
  2208.2 96.9 %collective-permute-start.12 = (f32[120,5120]{1,0:T(8,128)}, f32[120,5120]{1,0:T(8,128)}, u32[]{:S(2)}, u32[]{:S(2)}) collective-permute-start(f32[120,5120]{1,0:T(8,128)} %get-tuple-element.88), channel_id=1, source_target_pairs={{0,2},{1,3},{2,0},{3,1},{4,6},{5,7},{6,4},{7,5}} | collective-permute-start | bytes 7372808 | tf_op jit(solution)/shard_map/ppermute | solution.py:162
  2313.7 316.9 %all-gather.16.cloned.1.call-start = ((), (), s32[]{:S(2)}) async-start(), calls=%async_computation.7 | async-start | bytes 13271040 | tf_op jit(solution)/shard_map/all_gather | solution.py:224
  2441.8 35.5 %collective-permute-start.2 = (f32[72,5120]{1,0:T(8,128)}, f32[72,5120]{1,0:T(8,128)}, u32[]{:S(2)}, u32[]{:S(2)}) collective-permute-start(f32[72,5120]{1,0:T(8,128)} %get-tuple-element.102), channel_id=1, source_target_pairs={{0,2},{1,3},{2,0},{3,1},{4,6},{5,7},{6,4},{7,5}} | collective-permute-start | bytes 4423688 | tf_op jit(solution)/shard_map/ppermute | solution.py:162
  2442.2 35.5 %collective-permute-start.4 = (f32[72,5120]{1,0:T(8,128)}, f32[72,5120]{1,0:T(8,128)}, u32[]{:S(2)}, u32[]{:S(2)}) collective-permute-start(f32[72,5120]{1,0:T(8,128)} %get-tuple-element.101), channel_id=1, source_target_pairs={{0,4},{1,5},{2,6},{3,7},{4,0},{5,1},{6,2},{7,3}} | collective-permute-start | bytes 4423688 | tf_op jit(solution)/shard_map/ppermute | solution.py:162
  2442.4 66.5 %collective-permute-start.1 = (f32[72,5120]{1,0:T(8,128)}, f32[72,5120]{1,0:T(8,128)}, u32[]{:S(2)}, u32[]{:S(2)}) collective-permute-start(f32[72,5120]{1,0:T(8,128)} %get-tuple-element.99), channel_id=1, source_target_pairs={{0,2},{1,3},{2,0},{3,1},{4,6},{5,7},{6,4},{7,5}} | collective-permute-start | bytes 4423688 | tf_op jit(solution)/shard_map/ppermute | solution.py:162
  2443.9 65.4 %collective-permute-start.6 = (f32[72,5120]{1,0:T(8,128)S(1)}, f32[72,5120]{1,0:T(8,128)}, u32[]{:S(2)}, u32[]{:S(2)}) collective-permute-start(f32[72,5120]{1,0:T(8,128)S(1)} %get-tuple-element.100), channel_id=1, source_target_pairs={{0,4},{1,5},{2,6},{3,7},{4,0},{5,1},{6,2},{7,3}} | collective-permute-start | bytes 4423688 | tf_op jit(solution)/shard_map/ppermute | solution.py:162
  2482.5 57.3 %collective-permute-start.3 = (f32[72,5120]{1,0:T(8,128)}, f32[72,5120]{1,0:T(8,128)}, u32[]{:S(2)}, u32[]{:S(2)}) collective-permute-start(f32[72,5120]{1,0:T(8,128)} %get-tuple-element.103), channel_id=1, source_target_pairs={{0,4},{1,5},{2,6},{3,7},{4,0},{5,1},{6,2},{7,3}} | collective-permute-start | bytes 4423688 | tf_op jit(solution)/shard_map/ppermute | solution.py:162
  2482.7 57.1 %collective-permute-start.5 = (f32[72,5120]{1,0:T(8,128)}, f32[72,5120]{1,0:T(8,128)}, u32[]{:S(2)}, u32[]{:S(2)}) collective-permute-start(f32[72,5120]{1,0:T(8,128)} %get-tuple-element.104), channel_id=1, source_target_pairs={{0,2},{1,3},{2,0},{3,1},{4,6},{5,7},{6,4},{7,5}} | collective-permute-start | bytes 4423688 | tf_op jit(solution)/shard_map/ppermute | solution.py:162
  (33 other events, 735.3 us)
Sparse Core Ops, SparseCore 0:
  14.7 259.2 all-gather.11
  306.6 114.7 all-gather.29
  423.2 149.3 all-gather.25
  574.3 127.7 all-gather.21
  703.7 96.3 all-gather.17
  801.8 63.0 all-gather.13
  1405.2 79.1 all-gather.31
  1713.9 205.5 all-gather.27
  2017.9 114.5 all-gather.23
  2313.8 95.6 all-gather.19
  2545.7 63.2 all-gather.15
